TPU v7x, 64 devices: a 2x2x8 block of a 4x4x8 slice. The times are simulated.
64 devices in a mesh: dp: 4 (over x, y), cp: 16 (over z, core).
Axes of the slice: x: 2, y: 2, z: 8, core: 2. Of those that a mesh axis runs over, the one named last changes fastest.
The devices are a block of a 4x4x8 slice.
Arguments:
- hidden: bfloat16 [65536, 4096], P(('dp', 'cp')), parts along dimension 0
- w_q: bfloat16 [4096, 4, 128], replicated
- w_k: bfloat16 [4096, 1, 128], replicated
- w_v: bfloat16 [4096, 1, 128], replicated
- w_o: bfloat16 [4, 128, 4096], replicated
Outputs:
- output: bfloat16 [65536, 4096], P(('dp', 'cp')), parts along dimension 0
There are 4 independent parts. A program takes and returns all parts, laid end to end along the dimension named above; an argument that names none is the same for every part.
All inputs are finite; a program needn't handle non-finite values.
Results may differ from a plain program's by a relative error of at most 0.00412167.
Values are sent between devices in bfloat16 or wider.
A program may use at most 768 MiB of HBM per device.

v0:
```python
import jax
import jax.numpy as jnp
from jax import lax
from jax.sharding import PartitionSpec as P

WINDOW = 4096
ROPE_BASE = 10000.0


def rotate(values, positions, factor):
    half_dim = values.shape[-1] // 2
    inv_freq = 1.0 / (ROPE_BASE ** (jnp.arange(half_dim, dtype=jnp.float32) * (2.0 / values.shape[-1])))
    angles = positions.astype(jnp.float32)[..., None, None] * inv_freq
    cos_part = jnp.cos(angles)
    sin_part = jnp.sin(angles)
    first_half = values[..., :half_dim].astype(jnp.float32)
    second_half = values[..., half_dim:].astype(jnp.float32)
    rotated = jnp.concatenate([first_half * cos_part - second_half * sin_part, second_half * cos_part + first_half * sin_part], axis=-1)
    return (rotated * factor).astype(jnp.bfloat16)


def band_attention(queries, key_band, val_band, first_pos):
    chunk_len = queries.shape[1]
    band_len = key_band.shape[1] - chunk_len
    q_block = min(chunk_len, 128)
    key_span = band_len + q_block
    row_ids = jnp.arange(q_block)[:, None]
    col_ids = jnp.arange(key_span)[None, :]
    in_band = (col_ids > row_ids) & (col_ids <= row_ids + band_len)

    def one_block(block_id):
        row_start = block_id * q_block
        q_part = lax.dynamic_slice_in_dim(queries, row_start, q_block, axis=1)
        k_part = lax.dynamic_slice_in_dim(key_band, row_start, key_span, axis=1)
        v_part = lax.dynamic_slice_in_dim(val_band, row_start, key_span, axis=1)
        key_pos = first_pos[:, None] + row_start + jnp.arange(key_span)[None, :]
        allowed = in_band[None, :, :] & (key_pos >= 0)[:, None, :]
        scores = jnp.einsum('nqkgd,nskd->nkgqs', q_part, k_part, preferred_element_type=jnp.float32)
        scores = jnp.where(allowed[:, None, None, :, :], scores, -jnp.inf)
        row_max = jnp.max(scores, axis=-1, keepdims=True)
        exp_scores = jnp.exp(scores - row_max)
        row_sum = jnp.sum(exp_scores, axis=-1)
        attn_out = jnp.einsum('nkgqs,nskd->nqkgd', exp_scores.astype(jnp.bfloat16), v_part, preferred_element_type=jnp.float32)
        attn_out = attn_out / jnp.transpose(row_sum, (0, 3, 1, 2))[..., None]
        return attn_out.astype(jnp.bfloat16)

    blocks = lax.map(one_block, jnp.arange(chunk_len // q_block))
    return jnp.moveaxis(blocks, 0, 1).reshape(queries.shape)


def solution(mesh):
    cp_size = mesh.shape['cp']

    def device_step(hidden, w_q, w_k, w_v, w_o):
        my_index = lax.axis_index('cp')
        chunk_len = hidden.shape[0] // 2
        model_dim = hidden.shape[1]
        heads, head_dim = w_q.shape[1], w_q.shape[2]
        kv_heads = w_k.shape[1]
        group_size = heads // kv_heads
        win_chunks = WINDOW // chunk_len
        x_halves = hidden.reshape(2, chunk_len, model_dim)
        chunk_ids = jnp.stack([my_index, 2 * cp_size - 1 - my_index])
        positions = chunk_ids[:, None] * chunk_len + jnp.arange(chunk_len)[None, :]
        key_proj = jnp.einsum('nqd,dhe->nqhe', x_halves, w_k, preferred_element_type=jnp.float32).astype(jnp.bfloat16)
        val_proj = jnp.einsum('nqd,dhe->nqhe', x_halves, w_v, preferred_element_type=jnp.float32).astype(jnp.bfloat16)
        kv_pairs = jnp.stack([rotate(key_proj, positions, 1.0), val_proj], axis=1)
        kv_first = kv_pairs[0]
        kv_second = kv_pairs[1]
        from_below = []
        from_above = []
        from_fold = []
        for offset in range(1, win_chunks + 1):
            from_below.append(lax.ppermute(kv_first, 'cp', [(sender, sender + offset) for sender in range(cp_size - offset)]))
            from_above.append(lax.ppermute(kv_second, 'cp', [(sender, sender - offset) for sender in range(offset, cp_size)]))
            fold_pairs = [(sender, 2 * cp_size - 1 - sender - offset) for sender in range(cp_size - offset, cp_size) if 2 * cp_size - 1 - sender - offset != sender]
            if fold_pairs:
                from_fold.append(lax.ppermute(kv_first, 'cp', fold_pairs))
            else:
                from_fold.append(jnp.zeros_like(kv_first))
        upper_slots = []
        for offset in range(1, win_chunks + 1):
            fold_or_self = jnp.where(2 * cp_size - 1 - my_index - offset == my_index, kv_first, from_fold[offset - 1])
            upper_slots.append(jnp.where(my_index + offset < cp_size, from_above[offset - 1], fold_or_self))
        band_low = jnp.concatenate(from_below[::-1] + [kv_first], axis=1)
        band_high = jnp.concatenate(upper_slots[::-1] + [kv_second], axis=1)
        bands = jnp.stack([band_low, band_high], axis=1)
        q_proj = jnp.einsum('nqd,dhe->nqhe', x_halves, w_q, preferred_element_type=jnp.float32).astype(jnp.bfloat16)
        queries = rotate(q_proj, positions, head_dim ** -0.5).reshape(2, chunk_len, kv_heads, group_size, head_dim)
        first_pos = (chunk_ids - win_chunks) * chunk_len
        attended = band_attention(queries, bands[0], bands[1], first_pos)
        w_out = w_o.reshape(kv_heads, group_size, head_dim, model_dim)
        out_rows = jnp.einsum('nqkge,kgem->nqm', attended, w_out, preferred_element_type=jnp.float32)
        return out_rows.astype(jnp.bfloat16).reshape(2 * chunk_len, model_dim)

    return jax.shard_map(device_step, mesh=mesh, in_specs=(P(('dp', 'cp'), None), P(), P(), P(), P()), out_specs=P(('dp', 'cp'), None), check_vma=False)
```

profile of v0, /device:TPU:55, one launch (start us, length us, event | category | flops | bytes accessed | tf_op | source)
XLA Modules:
  0.0 317.4 jit_solution(1919983451701527307)
XLA Ops:
  1.2 6.4 %fusion.50 = bf16[2,512,1,128]{1,3,0,2:T(8,128)(2,1)S(1)} fusion(bf16[2,512,4096]{2,1,0:T(8,128)(2,1)} %bitcast.182, bf16[4096,1,128]{2,0,1:T(8,128)(2,1)S(1)} %copy-done), kind=kOutput, calls=%fused_computation.49 | convolution fusion | flops 1073872896 | bytes 9699328 | tf_op jit(solution)/shard_map/nqd,dhe->nqhe/dot_general | solution.py:65
  7.7 2.9 fusion.51
  10.6 1.2 fusion.67
  11.9 8.8 %collective-permute-start = (bf16[2,512,1,128]{1,3,0,2:T(8,128)(2,1)S(1)}, bf16[2,512,1,128]{1,3,0,2:T(8,128)(2,1)S(1)}, u32[]{:S(2)}, u32[]{:S(2)}) collective-permute-start(bf16[2,512,1,128]{1,3,0,2:T(8,128)(2,1)S(1)} %get-tuple-element.108), channel_id=1, source_target_pairs={{0,8},{1,9},{2,10},{3,11},{4,12},{5,13},{6,14},{7,15},{16,24},{17,... | collective-permute-start | bytes 786440 | tf_op jit(solution)/shard_map/ppermute | solution.py:74
  22.0 1.3 collective-permute-start.8
  23.3 1.3 collective-permute-start.10
  25.6 7.4 %copy.17 = bf16[4096,4,128]{0,2,1:T(8,128)(2,1)} copy(bf16[4096,4,128]{2,1,0:T(4,128)(2,1)} %param.8) | data formatting | bytes 8388608 | tf_op args[1]
  33.1 9.1 %fusion.47 = bf16[2,512,4,128]{1,3,2,0:T(8,128)(2,1)S(1)} fusion(bf16[2,512,4096,1]{2,1,3,0:T(8,128)(2,1)} %bitcast.183, bf16[4096,4,128]{0,2,1:T(8,128)(2,1)} %copy.17), kind=kOutput, calls=%fused_computation.42 | convolution fusion | flops 4295491584 | bytes 13631488 | tf_op jit(solution)/shard_map/nqd,dhe->nqhe/dot_general | solution.py:88
  43.6 1.3 collective-permute-start.12
  45.7 13.8 %collective-permute-done.10 = bf16[2,512,1,128]{1,3,0,2:T(8,128)(2,1)S(1)} collective-permute-done((bf16[2,512,1,128]{1,3,0,2:T(8,128)(2,1)S(1)}, bf16[2,512,1,128]{1,3,0,2:T(8,128)(2,1)S(1)}, u32[]{:S(2)}, u32[]{:S(2)}) %collective-permute-start.10) | collective-permute-done | bytes 262176 | tf_op jit(solution)/shard_map/ppermute | solution.py:75
  59.5 1.3 collective-permute-start.14
  61.6 8.4 %collective-permute-done.12 = bf16[2,512,1,128]{1,3,0,2:T(8,128)(2,1)S(1)} collective-permute-done((bf16[2,512,1,128]{1,3,0,2:T(8,128)(2,1)S(1)}, bf16[2,512,1,128]{1,3,0,2:T(8,128)(2,1)S(1)}, u32[]{:S(2)}, u32[]{:S(2)}) %collective-permute-start.12) | collective-permute-done | bytes 262176 | tf_op jit(solution)/shard_map/ppermute | solution.py:75
  70.0 1.5 collective-permute-start.16
  72.3 11.7 %collective-permute-done.14 = bf16[2,512,1,128]{1,3,0,2:T(8,128)(2,1)S(1)} collective-permute-done((bf16[2,512,1,128]{1,3,0,2:T(8,128)(2,1)S(1)}, bf16[2,512,1,128]{1,3,0,2:T(8,128)(2,1)S(1)}, u32[]{:S(2)}, u32[]{:S(2)}) %collective-permute-start.14) | collective-permute-done | bytes 262176 | tf_op jit(solution)/shard_map/ppermute | solution.py:75
  84.0 1.9 collective-permute-start.18
  86.1 20.0 %collective-permute-start.1 = (bf16[2,512,1,128]{1,3,0,2:T(8,128)(2,1)S(1)}, bf16[2,512,1,128]{1,3,0,2:T(8,128)(2,1)S(1)}, u32[]{:S(2)}, u32[]{:S(2)}) collective-permute-start(bf16[2,512,1,128]{1,3,0,2:T(8,128)(2,1)S(1)} %get-tuple-element.108), channel_id=1, source_target_pairs={{0,7},{1,8},{2,9},{3,10},{4,11},{5,12},{6,13},{7,14},{8,15},{16,23... | collective-permute-start | bytes 786440 | tf_op jit(solution)/shard_map/ppermute | solution.py:74
  106.1 5.1 %collective-permute-start.2 = (bf16[2,512,1,128]{1,3,0,2:T(8,128)(2,1)S(1)}, bf16[2,512,1,128]{1,3,0,2:T(8,128)(2,1)S(1)}, u32[]{:S(2)}, u32[]{:S(2)}) collective-permute-start(bf16[2,512,1,128]{1,3,0,2:T(8,128)(2,1)S(1)} %get-tuple-element.108), channel_id=1, source_target_pairs={{0,6},{1,7},{2,8},{3,9},{4,10},{5,11},{6,12},{7,13},{8,14},{9,15},... | collective-permute-start | bytes 786440 | tf_op jit(solution)/shard_map/ppermute | solution.py:74
  111.4 1.3 collective-permute-start.3
  112.7 6.1 %collective-permute-start.4 = (bf16[2,512,1,128]{1,3,0,2:T(8,128)(2,1)S(1)}, bf16[2,512,1,128]{1,3,0,2:T(8,128)(2,1)S(1)}, u32[]{:S(2)}, u32[]{:S(2)}) collective-permute-start(bf16[2,512,1,128]{1,3,0,2:T(8,128)(2,1)S(1)} %get-tuple-element.108), channel_id=1, source_target_pairs={{0,4},{1,5},{2,6},{3,7},{4,8},{5,9},{6,10},{7,11},{8,12},{9,13},{1... | collective-permute-start | bytes 786440 | tf_op jit(solution)/shard_map/ppermute | solution.py:74
  119.0 2.6 collective-permute-start.5
  121.7 7.4 %collective-permute-start.6 = (bf16[2,512,1,128]{1,3,0,2:T(8,128)(2,1)S(1)}, bf16[2,512,1,128]{1,3,0,2:T(8,128)(2,1)S(1)}, u32[]{:S(2)}, u32[]{:S(2)}) collective-permute-start(bf16[2,512,1,128]{1,3,0,2:T(8,128)(2,1)S(1)} %get-tuple-element.108), channel_id=1, source_target_pairs={{0,2},{1,3},{2,4},{3,5},{4,6},{5,7},{6,8},{7,9},{8,10},{9,11},{10,... | collective-permute-start | bytes 786440 | tf_op jit(solution)/shard_map/ppermute | solution.py:74
  129.1 7.9 %collective-permute-done.2 = bf16[2,512,1,128]{1,3,0,2:T(8,128)(2,1)S(1)} collective-permute-done((bf16[2,512,1,128]{1,3,0,2:T(8,128)(2,1)S(1)}, bf16[2,512,1,128]{1,3,0,2:T(8,128)(2,1)S(1)}, u32[]{:S(2)}, u32[]{:S(2)}) %collective-permute-start.2) | collective-permute-done | bytes 262176 | tf_op jit(solution)/shard_map/ppermute | solution.py:74
  137.0 15.8 %collective-permute-start.7 = (bf16[2,512,1,128]{1,3,0,2:T(8,128)(2,1)S(1)}, bf16[2,512,1,128]{1,3,0,2:T(8,128)(2,1)S(1)}, u32[]{:S(2)}, u32[]{:S(2)}) collective-permute-start(bf16[2,512,1,128]{1,3,0,2:T(8,128)(2,1)S(1)} %get-tuple-element.108), channel_id=1, source_target_pairs={{0,1},{1,2},{2,3},{3,4},{4,5},{5,6},{6,7},{7,8},{8,9},{9,10},{10,1... | collective-permute-start | bytes 786440 | tf_op jit(solution)/shard_map/ppermute | solution.py:74
  153.5 2.0 collective-permute-start.20
  155.5 2.0 collective-permute-start.22
  157.5 1.6 collective-permute-done.6
  159.2 2.8 collective-permute-done.7
  162.0 8.2 %collective-permute-done.20 = bf16[2,512,1,128]{1,3,0,2:T(8,128)(2,1)S(1)} collective-permute-done((bf16[2,512,1,128]{1,3,0,2:T(8,128)(2,1)S(1)}, bf16[2,512,1,128]{1,3,0,2:T(8,128)(2,1)S(1)}, u32[]{:S(2)}, u32[]{:S(2)}) %collective-permute-start.20) | collective-permute-done | bytes 262176 | tf_op jit(solution)/shard_map/ppermute | solution.py:75
  170.3 5.6 %collective-permute-done.22 = bf16[2,512,1,128]{1,3,0,2:T(8,128)(2,1)S(1)} collective-permute-done((bf16[2,512,1,128]{1,3,0,2:T(8,128)(2,1)S(1)}, bf16[2,512,1,128]{1,3,0,2:T(8,128)(2,1)S(1)}, u32[]{:S(2)}, u32[]{:S(2)}) %collective-permute-start.22) | collective-permute-done | bytes 262176 | tf_op jit(solution)/shard_map/ppermute | solution.py:75
  176.1 2.4 fusion.45
  178.5 130.2 %while.11 = (s32[]{:T(128)}, bf16[4,2,128,1,4,128]{5,2,0,4,1,3:T(8,128)(2,1)}, s32[4]{0:T(128)S(1)}, bf16[2,4608,1,128]{1,3,0,2:T(8,128)(2,1)}, s32[2]{0:T(128)S...) while((s32[]{:T(128)}, ...), condition=%wide.region_3.4_spmd.clone, body=%wide.region_0.3_spmd.clone.sunk | while | flops 2252175872 | bytes 63248120 | solution.py:47
  180.3 1.7 broadcast_and_fusion.2
  181.9 8.9 %fusion.81 = (f32[2,4,128]{2,1,0:T(4,128)S(1)}, f32[2,4224,128,4]{2,1,3,0:T(8,128)}) fusion(pred[2,128,4224]{1,2,0:T(8,128)(4,1)S(1)} %broadcast_and_fusion.2, bf16[2,512,1,4,128]{1,4,3,0,2:T(8,128)(2,1)S(1)} %get-tuple-element.200, s32[]{:T(128)S(6)} %select_n.212, bf16[2,4608,1,128]{1,3,0,2:T(8,128)(2,1)} %get-tuple-element.199, s32[]{:T(128)S(6)} %select_n.213), kind=kOutput, calls=%fused_computation.3.clone.1 | convolution fusion | flops 1115945984 | bytes 20811784 | tf_op jit(solution)/shard_map/while/body/eval_jaxpr/nqkgd,nskd->nkgqs/dot_general | solution.py:38
  190.9 9.0 %fusion.82 = f32[2,4,128]{2,1,0:T(4,128)S(1)} fusion(f32[2,4224,128,4]{2,1,3,0:T(8,128)} %get-tuple-element.166, f32[2,4,128]{2,1,0:T(4,128)S(1)} %get-tuple-element.167, pred[2,128,4224]{1,2,0:T(8,128)(4,1)S(1)} %broadcast_and_fusion.2), kind=kLoop, calls=%fused_computation.4.clone.1 | loop fusion | flops 12975104 | bytes 18391040 | tf_op jit(solution)/shard_map/while/body/eval_jaxpr/reduce_sum | solution.py:42
  199.9 10.2 %fusion.83 = bf16[1,2,128,1,4,128]{2,5,4,1,3,0:T(8,128)(2,1)S(1)} fusion(f32[2,4224,128,4]{2,1,3,0:T(8,128)} %get-tuple-element.166, f32[2,4,128]{2,1,0:T(4,128)S(1)} %get-tuple-element.167, pred[2,128,4224]{1,2,0:T(8,128)(4,1)S(1)} %broadcast_and_fusion.2, bf16[2,4608,1,128]{1,3,0,2:T(8,128)(2,1)} %get-tuple-element.197, s32[]{:T(128)S(6)} %select_n.213, ...), kind=kOutput, calls=%fused_computation.21.clone.1 | convolution fusion | flops 1120534528 | bytes 20815876 | tf_op jit(solution)/shard_map/while/body/eval_jaxpr/nkgqs,nskd->nqkgd/dot_general | solution.py:43
  212.8 1.7 broadcast_and_fusion.2
  214.5 8.9 %fusion.81 = (f32[2,4,128]{2,1,0:T(4,128)S(1)}, f32[2,4224,128,4]{2,1,3,0:T(8,128)}) fusion(pred[2,128,4224]{1,2,0:T(8,128)(4,1)S(1)} %broadcast_and_fusion.2, bf16[2,512,1,4,128]{1,4,3,0,2:T(8,128)(2,1)S(1)} %get-tuple-element.200, s32[]{:T(128)S(6)} %select_n.212, bf16[2,4608,1,128]{1,3,0,2:T(8,128)(2,1)} %get-tuple-element.199, s32[]{:T(128)S(6)} %select_n.213), kind=kOutput, calls=%fused_computation.3.clone.1 | convolution fusion | flops 1115945984 | bytes 20811784 | tf_op jit(solution)/shard_map/while/body/eval_jaxpr/nqkgd,nskd->nkgqs/dot_general | solution.py:38
  223.4 9.0 %fusion.82 = f32[2,4,128]{2,1,0:T(4,128)S(1)} fusion(f32[2,4224,128,4]{2,1,3,0:T(8,128)} %get-tuple-element.166, f32[2,4,128]{2,1,0:T(4,128)S(1)} %get-tuple-element.167, pred[2,128,4224]{1,2,0:T(8,128)(4,1)S(1)} %broadcast_and_fusion.2), kind=kLoop, calls=%fused_computation.4.clone.1 | loop fusion | flops 12975104 | bytes 18391040 | tf_op jit(solution)/shard_map/while/body/eval_jaxpr/reduce_sum | solution.py:42
  232.4 10.2 %fusion.83 = bf16[1,2,128,1,4,128]{2,5,4,1,3,0:T(8,128)(2,1)S(1)} fusion(f32[2,4224,128,4]{2,1,3,0:T(8,128)} %get-tuple-element.166, f32[2,4,128]{2,1,0:T(4,128)S(1)} %get-tuple-element.167, pred[2,128,4224]{1,2,0:T(8,128)(4,1)S(1)} %broadcast_and_fusion.2, bf16[2,4608,1,128]{1,3,0,2:T(8,128)(2,1)} %get-tuple-element.197, s32[]{:T(128)S(6)} %select_n.213, ...), kind=kOutput, calls=%fused_computation.21.clone.1 | convolution fusion | flops 1120534528 | bytes 20815876 | tf_op jit(solution)/shard_map/while/body/eval_jaxpr/nkgqs,nskd->nqkgd/dot_general | solution.py:43
  245.4 1.7 broadcast_and_fusion.2
  247.1 8.9 %fusion.81 = (f32[2,4,128]{2,1,0:T(4,128)S(1)}, f32[2,4224,128,4]{2,1,3,0:T(8,128)}) fusion(pred[2,128,4224]{1,2,0:T(8,128)(4,1)S(1)} %broadcast_and_fusion.2, bf16[2,512,1,4,128]{1,4,3,0,2:T(8,128)(2,1)S(1)} %get-tuple-element.200, s32[]{:T(128)S(6)} %select_n.212, bf16[2,4608,1,128]{1,3,0,2:T(8,128)(2,1)} %get-tuple-element.199, s32[]{:T(128)S(6)} %select_n.213), kind=kOutput, calls=%fused_computation.3.clone.1 | convolution fusion | flops 1115945984 | bytes 20811784 | tf_op jit(solution)/shard_map/while/body/eval_jaxpr/nqkgd,nskd->nkgqs/dot_general | solution.py:38
  256.0 9.0 %fusion.82 = f32[2,4,128]{2,1,0:T(4,128)S(1)} fusion(f32[2,4224,128,4]{2,1,3,0:T(8,128)} %get-tuple-element.166, f32[2,4,128]{2,1,0:T(4,128)S(1)} %get-tuple-element.167, pred[2,128,4224]{1,2,0:T(8,128)(4,1)S(1)} %broadcast_and_fusion.2), kind=kLoop, calls=%fused_computation.4.clone.1 | loop fusion | flops 12975104 | bytes 18391040 | tf_op jit(solution)/shard_map/while/body/eval_jaxpr/reduce_sum | solution.py:42
  265.0 10.2 %fusion.83 = bf16[1,2,128,1,4,128]{2,5,4,1,3,0:T(8,128)(2,1)S(1)} fusion(f32[2,4224,128,4]{2,1,3,0:T(8,128)} %get-tuple-element.166, f32[2,4,128]{2,1,0:T(4,128)S(1)} %get-tuple-element.167, pred[2,128,4224]{1,2,0:T(8,128)(4,1)S(1)} %broadcast_and_fusion.2, bf16[2,4608,1,128]{1,3,0,2:T(8,128)(2,1)} %get-tuple-element.197, s32[]{:T(128)S(6)} %select_n.213, ...), kind=kOutput, calls=%fused_computation.21.clone.1 | convolution fusion | flops 1120534528 | bytes 20815876 | tf_op jit(solution)/shard_map/while/body/eval_jaxpr/nkgqs,nskd->nqkgd/dot_general | solution.py:43
  277.9 1.7 broadcast_and_fusion.2
  279.6 8.9 %fusion.81 = (f32[2,4,128]{2,1,0:T(4,128)S(1)}, f32[2,4224,128,4]{2,1,3,0:T(8,128)}) fusion(pred[2,128,4224]{1,2,0:T(8,128)(4,1)S(1)} %broadcast_and_fusion.2, bf16[2,512,1,4,128]{1,4,3,0,2:T(8,128)(2,1)S(1)} %get-tuple-element.200, s32[]{:T(128)S(6)} %select_n.212, bf16[2,4608,1,128]{1,3,0,2:T(8,128)(2,1)} %get-tuple-element.199, s32[]{:T(128)S(6)} %select_n.213), kind=kOutput, calls=%fused_computation.3.clone.1 | convolution fusion | flops 1115945984 | bytes 20811784 | tf_op jit(solution)/shard_map/while/body/eval_jaxpr/nqkgd,nskd->nkgqs/dot_general | solution.py:38
  288.5 9.0 %fusion.82 = f32[2,4,128]{2,1,0:T(4,128)S(1)} fusion(f32[2,4224,128,4]{2,1,3,0:T(8,128)} %get-tuple-element.166, f32[2,4,128]{2,1,0:T(4,128)S(1)} %get-tuple-element.167, pred[2,128,4224]{1,2,0:T(8,128)(4,1)S(1)} %broadcast_and_fusion.2), kind=kLoop, calls=%fused_computation.4.clone.1 | loop fusion | flops 12975104 | bytes 18391040 | tf_op jit(solution)/shard_map/while/body/eval_jaxpr/reduce_sum | solution.py:42
  297.5 10.2 %fusion.83 = bf16[1,2,128,1,4,128]{2,5,4,1,3,0:T(8,128)(2,1)S(1)} fusion(f32[2,4224,128,4]{2,1,3,0:T(8,128)} %get-tuple-element.166, f32[2,4,128]{2,1,0:T(4,128)S(1)} %get-tuple-element.167, pred[2,128,4224]{1,2,0:T(8,128)(4,1)S(1)} %broadcast_and_fusion.2, bf16[2,4608,1,128]{1,3,0,2:T(8,128)(2,1)} %get-tuple-element.197, s32[]{:T(128)S(6)} %select_n.213, ...), kind=kOutput, calls=%fused_computation.21.clone.1 | convolution fusion | flops 1120534528 | bytes 20815876 | tf_op jit(solution)/shard_map/while/body/eval_jaxpr/nkgqs,nskd->nqkgd/dot_general | solution.py:43
  308.7 8.7 %bitcast_convert_fusion = bf16[2,512,4096]{2,1,0:T(8,128)(2,1)} fusion(bf16[2,512,4,128]{3,1,2,0:T(8,128)(2,1)} %bitcast.188, bf16[4,128,4096]{2,1,0:T(8,128)(2,1)} %param.11), kind=kOutput, calls=%fused_computation.30 | convolution fusion | flops 4299161600 | bytes 13631488 | tf_op jit(solution)/shard_map/nqkge,kgem->nqm/dot_general | solution.py:93
  (82 shorter events, 17.1 us)
Async XLA Ops:
  0.0 1.2 copy-start
  1.2 6.4 %copy-start.2 = (bf16[1024,4096]{1,0:T(8,128)(2,1)S(1)}, bf16[1024,4096]{1,0:T(8,128)(2,1)}, u32[]{:S(2)}) copy-start(bf16[1024,4096]{1,0:T(8,128)(2,1)} %param.7) | copy-start | bytes 25165828
  1.2 6.5 %copy-start.3 = (bf16[4096,1,128]{2,0,1:T(8,128)(2,1)S(1)}, bf16[4096,1,128]{2,0,1:T(8,128)(2,1)}, u32[]{:S(2)}) copy-start(bf16[4096,1,128]{2,0,1:T(8,128)(2,1)} %param.10) | copy-start | bytes 3145732
  11.9 107.1 %collective-permute-start = (bf16[2,512,1,128]{1,3,0,2:T(8,128)(2,1)S(1)}, bf16[2,512,1,128]{1,3,0,2:T(8,128)(2,1)S(1)}, u32[]{:S(2)}, u32[]{:S(2)}) collective-permute-start(bf16[2,512,1,128]{1,3,0,2:T(8,128)(2,1)S(1)} %get-tuple-element.108), channel_id=1, source_target_pairs={{0,8},{1,9},{2,10},{3,11},{4,12},{5,13},{6,14},{7,15},{16,24},{17,... | collective-permute-start | bytes 786440 | tf_op jit(solution)/shard_map/ppermute | solution.py:74
  20.6 22.2 %collective-permute-start.9 = (bf16[2,512,1,128]{1,3,0,2:T(8,128)(2,1)S(1)}, bf16[2,512,1,128]{1,3,0,2:T(8,128)(2,1)S(1)}, u32[]{:S(2)}, u32[]{:S(2)}) collective-permute-start(bf16[2,512,1,128]{1,3,0,2:T(8,128)(2,1)S(1)} %get-tuple-element.108), channel_id=1, source_target_pairs={{8,15},{9,14},{10,13},{11,12},{12,11},{13,10},{14,9},{15,8},{24,31... | collective-permute-start | bytes 786440 | tf_op jit(solution)/shard_map/ppermute | solution.py:78
  21.3 23.7 %collective-permute-start.11 = (bf16[2,512,1,128]{1,3,0,2:T(8,128)(2,1)S(1)}, bf16[2,512,1,128]{1,3,0,2:T(8,128)(2,1)S(1)}, u32[]{:S(2)}, u32[]{:S(2)}) collective-permute-start(bf16[2,512,1,128]{1,3,0,2:T(8,128)(2,1)S(1)} %get-tuple-element.108), channel_id=1, source_target_pairs={{9,15},{10,14},{11,13},{13,11},{14,10},{15,9},{25,31},{26,30},{27,... | collective-permute-start | bytes 786440 | tf_op jit(solution)/shard_map/ppermute | solution.py:78
  22.0 21.6 %collective-permute-start.8 = (bf16[2,512,1,128]{1,3,0,2:T(8,128)(2,1)S(1)}, bf16[2,512,1,128]{1,3,0,2:T(8,128)(2,1)S(1)}, u32[]{:S(2)}, u32[]{:S(2)}) collective-permute-start(bf16[2,512,1,128]{1,3,0,2:T(8,128)(2,1)S(1)} %get-tuple-element.107), channel_id=1, source_target_pairs={{8,0},{9,1},{10,2},{11,3},{12,4},{13,5},{14,6},{15,7},{24,16},{25,... | collective-permute-start | bytes 786440 | tf_op jit(solution)/shard_map/ppermute | solution.py:75
  23.3 36.2 %collective-permute-start.10 = (bf16[2,512,1,128]{1,3,0,2:T(8,128)(2,1)S(1)}, bf16[2,512,1,128]{1,3,0,2:T(8,128)(2,1)S(1)}, u32[]{:S(2)}, u32[]{:S(2)}) collective-permute-start(bf16[2,512,1,128]{1,3,0,2:T(8,128)(2,1)S(1)} %get-tuple-element.107), channel_id=1, source_target_pairs={{7,0},{8,1},{9,2},{10,3},{11,4},{12,5},{13,6},{14,7},{15,8},{23,16... | collective-permute-start | bytes 786440 | tf_op jit(solution)/shard_map/ppermute | solution.py:75
  42.9 18.0 %collective-permute-start.13 = (bf16[2,512,1,128]{1,3,0,2:T(8,128)(2,1)S(1)}, bf16[2,512,1,128]{1,3,0,2:T(8,128)(2,1)S(1)}, u32[]{:S(2)}, u32[]{:S(2)}) collective-permute-start(bf16[2,512,1,128]{1,3,0,2:T(8,128)(2,1)S(1)} %get-tuple-element.108), channel_id=1, source_target_pairs={{10,15},{11,14},{12,13},{13,12},{14,11},{15,10},{26,31},{27,30},{2... | collective-permute-start | bytes 786440 | tf_op jit(solution)/shard_map/ppermute | solution.py:78
  43.6 26.5 %collective-permute-start.12 = (bf16[2,512,1,128]{1,3,0,2:T(8,128)(2,1)S(1)}, bf16[2,512,1,128]{1,3,0,2:T(8,128)(2,1)S(1)}, u32[]{:S(2)}, u32[]{:S(2)}) collective-permute-start(bf16[2,512,1,128]{1,3,0,2:T(8,128)(2,1)S(1)} %get-tuple-element.107), channel_id=1, source_target_pairs={{6,0},{7,1},{8,2},{9,3},{10,4},{11,5},{12,6},{13,7},{14,8},{15,9},... | collective-permute-start | bytes 786440 | tf_op jit(solution)/shard_map/ppermute | solution.py:75
  45.0 26.6 %collective-permute-start.15 = (bf16[2,512,1,128]{1,3,0,2:T(8,128)(2,1)S(1)}, bf16[2,512,1,128]{1,3,0,2:T(8,128)(2,1)S(1)}, u32[]{:S(2)}, u32[]{:S(2)}) collective-permute-start(bf16[2,512,1,128]{1,3,0,2:T(8,128)(2,1)S(1)} %get-tuple-element.108), channel_id=1, source_target_pairs={{11,15},{12,14},{14,12},{15,11},{27,31},{28,30},{30,28},{31,27},{4... | collective-permute-start | bytes 786440 | tf_op jit(solution)/shard_map/ppermute | solution.py:78
  59.5 24.5 %collective-permute-start.14 = (bf16[2,512,1,128]{1,3,0,2:T(8,128)(2,1)S(1)}, bf16[2,512,1,128]{1,3,0,2:T(8,128)(2,1)S(1)}, u32[]{:S(2)}, u32[]{:S(2)}) collective-permute-start(bf16[2,512,1,128]{1,3,0,2:T(8,128)(2,1)S(1)} %get-tuple-element.107), channel_id=1, source_target_pairs={{5,0},{6,1},{7,2},{8,3},{9,4},{10,5},{11,6},{12,7},{13,8},{14,9},{... | collective-permute-start | bytes 786440 | tf_op jit(solution)/shard_map/ppermute | solution.py:75
  60.9 25.2 %collective-permute-start.17 = (bf16[2,512,1,128]{1,3,0,2:T(8,128)(2,1)S(1)}, bf16[2,512,1,128]{1,3,0,2:T(8,128)(2,1)S(1)}, u32[]{:S(2)}, u32[]{:S(2)}) collective-permute-start(bf16[2,512,1,128]{1,3,0,2:T(8,128)(2,1)S(1)} %get-tuple-element.108), channel_id=1, source_target_pairs={{12,15},{13,14},{14,13},{15,12},{28,31},{29,30},{30,29},{31,28},{4... | collective-permute-start | bytes 786440 | tf_op jit(solution)/shard_map/ppermute | solution.py:78
  70.0 36.1 %collective-permute-start.16 = (bf16[2,512,1,128]{1,3,0,2:T(8,128)(2,1)S(1)}, bf16[2,512,1,128]{1,3,0,2:T(8,128)(2,1)S(1)}, u32[]{:S(2)}, u32[]{:S(2)}) collective-permute-start(bf16[2,512,1,128]{1,3,0,2:T(8,128)(2,1)S(1)} %get-tuple-element.107), channel_id=1, source_target_pairs={{4,0},{5,1},{6,2},{7,3},{8,4},{9,5},{10,6},{11,7},{12,8},{13,9},{1... | collective-permute-start | bytes 786440 | tf_op jit(solution)/shard_map/ppermute | solution.py:75
  71.7 39.7 %collective-permute-start.19 = (bf16[2,512,1,128]{1,3,0,2:T(8,128)(2,1)S(1)}, bf16[2,512,1,128]{1,3,0,2:T(8,128)(2,1)S(1)}, u32[]{:S(2)}, u32[]{:S(2)}) collective-permute-start(bf16[2,512,1,128]{1,3,0,2:T(8,128)(2,1)S(1)} %get-tuple-element.108), channel_id=1, source_target_pairs={{13,15},{15,13},{29,31},{31,29},{45,47},{47,45},{61,63},{63,61}} | collective-permute-start | bytes 786440 | tf_op jit(solution)/shard_map/ppermute | solution.py:78
  84.0 28.7 %collective-permute-start.18 = (bf16[2,512,1,128]{1,3,0,2:T(8,128)(2,1)S(1)}, bf16[2,512,1,128]{1,3,0,2:T(8,128)(2,1)S(1)}, u32[]{:S(2)}, u32[]{:S(2)}) collective-permute-start(bf16[2,512,1,128]{1,3,0,2:T(8,128)(2,1)S(1)} %get-tuple-element.107), channel_id=1, source_target_pairs={{3,0},{4,1},{5,2},{6,3},{7,4},{8,5},{9,6},{10,7},{11,8},{12,9},{13... | collective-permute-start | bytes 786440 | tf_op jit(solution)/shard_map/ppermute | solution.py:75
  86.1 35.5 %collective-permute-start.1 = (bf16[2,512,1,128]{1,3,0,2:T(8,128)(2,1)S(1)}, bf16[2,512,1,128]{1,3,0,2:T(8,128)(2,1)S(1)}, u32[]{:S(2)}, u32[]{:S(2)}) collective-permute-start(bf16[2,512,1,128]{1,3,0,2:T(8,128)(2,1)S(1)} %get-tuple-element.108), channel_id=1, source_target_pairs={{0,7},{1,8},{2,9},{3,10},{4,11},{5,12},{6,13},{7,14},{8,15},{16,23... | collective-permute-start | bytes 786440 | tf_op jit(solution)/shard_map/ppermute | solution.py:74
  106.1 30.8 %collective-permute-start.2 = (bf16[2,512,1,128]{1,3,0,2:T(8,128)(2,1)S(1)}, bf16[2,512,1,128]{1,3,0,2:T(8,128)(2,1)S(1)}, u32[]{:S(2)}, u32[]{:S(2)}) collective-permute-start(bf16[2,512,1,128]{1,3,0,2:T(8,128)(2,1)S(1)} %get-tuple-element.108), channel_id=1, source_target_pairs={{0,6},{1,7},{2,8},{3,9},{4,10},{5,11},{6,12},{7,13},{8,14},{9,15},... | collective-permute-start | bytes 786440 | tf_op jit(solution)/shard_map/ppermute | solution.py:74
  111.4 41.4 %collective-permute-start.3 = (bf16[2,512,1,128]{1,3,0,2:T(8,128)(2,1)S(1)}, bf16[2,512,1,128]{1,3,0,2:T(8,128)(2,1)S(1)}, u32[]{:S(2)}, u32[]{:S(2)}) collective-permute-start(bf16[2,512,1,128]{1,3,0,2:T(8,128)(2,1)S(1)} %get-tuple-element.108), channel_id=1, source_target_pairs={{0,5},{1,6},{2,7},{3,8},{4,9},{5,10},{6,11},{7,12},{8,13},{9,14},{... | collective-permute-start | bytes 786440 | tf_op jit(solution)/shard_map/ppermute | solution.py:74
  112.7 40.8 %collective-permute-start.4 = (bf16[2,512,1,128]{1,3,0,2:T(8,128)(2,1)S(1)}, bf16[2,512,1,128]{1,3,0,2:T(8,128)(2,1)S(1)}, u32[]{:S(2)}, u32[]{:S(2)}) collective-permute-start(bf16[2,512,1,128]{1,3,0,2:T(8,128)(2,1)S(1)} %get-tuple-element.108), channel_id=1, source_target_pairs={{0,4},{1,5},{2,6},{3,7},{4,8},{5,9},{6,10},{7,11},{8,12},{9,13},{1... | collective-permute-start | bytes 786440 | tf_op jit(solution)/shard_map/ppermute | solution.py:74
  119.0 36.5 %collective-permute-start.5 = (bf16[2,512,1,128]{1,3,0,2:T(8,128)(2,1)S(1)}, bf16[2,512,1,128]{1,3,0,2:T(8,128)(2,1)S(1)}, u32[]{:S(2)}, u32[]{:S(2)}) collective-permute-start(bf16[2,512,1,128]{1,3,0,2:T(8,128)(2,1)S(1)} %get-tuple-element.108), channel_id=1, source_target_pairs={{0,3},{1,4},{2,5},{3,6},{4,7},{5,8},{6,9},{7,10},{8,11},{9,12},{10... | collective-permute-start | bytes 786440 | tf_op jit(solution)/shard_map/ppermute | solution.py:74
  121.7 37.5 %collective-permute-start.6 = (bf16[2,512,1,128]{1,3,0,2:T(8,128)(2,1)S(1)}, bf16[2,512,1,128]{1,3,0,2:T(8,128)(2,1)S(1)}, u32[]{:S(2)}, u32[]{:S(2)}) collective-permute-start(bf16[2,512,1,128]{1,3,0,2:T(8,128)(2,1)S(1)} %get-tuple-element.108), channel_id=1, source_target_pairs={{0,2},{1,3},{2,4},{3,5},{4,6},{5,7},{6,8},{7,9},{8,10},{9,11},{10,... | collective-permute-start | bytes 786440 | tf_op jit(solution)/shard_map/ppermute | solution.py:74
  137.0 25.0 %collective-permute-start.7 = (bf16[2,512,1,128]{1,3,0,2:T(8,128)(2,1)S(1)}, bf16[2,512,1,128]{1,3,0,2:T(8,128)(2,1)S(1)}, u32[]{:S(2)}, u32[]{:S(2)}) collective-permute-start(bf16[2,512,1,128]{1,3,0,2:T(8,128)(2,1)S(1)} %get-tuple-element.108), channel_id=1, source_target_pairs={{0,1},{1,2},{2,3},{3,4},{4,5},{5,6},{6,7},{7,8},{8,9},{9,10},{10,1... | collective-permute-start | bytes 786440 | tf_op jit(solution)/shard_map/ppermute | solution.py:74
  152.8 9.2 %collective-permute-start.21 = (bf16[2,512,1,128]{1,3,0,2:T(8,128)(2,1)S(1)}, bf16[2,512,1,128]{1,3,0,2:T(8,128)(2,1)S(1)}, u32[]{:S(2)}, u32[]{:S(2)}) collective-permute-start(bf16[2,512,1,128]{1,3,0,2:T(8,128)(2,1)S(1)} %get-tuple-element.108), channel_id=1, source_target_pairs={{14,15},{15,14},{30,31},{31,30},{46,47},{47,46},{62,63},{63,62}} | collective-permute-start | bytes 786440 | tf_op jit(solution)/shard_map/ppermute | solution.py:78
  153.5 16.7 %collective-permute-start.20 = (bf16[2,512,1,128]{1,3,0,2:T(8,128)(2,1)S(1)}, bf16[2,512,1,128]{1,3,0,2:T(8,128)(2,1)S(1)}, u32[]{:S(2)}, u32[]{:S(2)}) collective-permute-start(bf16[2,512,1,128]{1,3,0,2:T(8,128)(2,1)S(1)} %get-tuple-element.107), channel_id=1, source_target_pairs={{2,0},{3,1},{4,2},{5,3},{6,4},{7,5},{8,6},{9,7},{10,8},{11,9},{12,... | collective-permute-start | bytes 786440 | tf_op jit(solution)/shard_map/ppermute | solution.py:75
  155.5 20.4 %collective-permute-start.22 = (bf16[2,512,1,128]{1,3,0,2:T(8,128)(2,1)S(1)}, bf16[2,512,1,128]{1,3,0,2:T(8,128)(2,1)S(1)}, u32[]{:S(2)}, u32[]{:S(2)}) collective-permute-start(bf16[2,512,1,128]{1,3,0,2:T(8,128)(2,1)S(1)} %get-tuple-element.107), channel_id=1, source_target_pairs={{1,0},{2,1},{3,2},{4,3},{5,4},{6,5},{7,6},{8,7},{9,8},{10,9},{11,1... | collective-permute-start | bytes 786440 | tf_op jit(solution)/shard_map/ppermute | solution.py:75
  308.7 8.7 %copy-start.1 = (bf16[4096,1,128]{2,0,1:T(8,128)(2,1)S(1)}, bf16[4096,1,128]{2,0,1:T(8,128)(2,1)}, u32[]{:S(2)}) copy-start(bf16[4096,1,128]{2,0,1:T(8,128)(2,1)} %param.9) | copy-start | bytes 3145732
where the time goes:
time: 320 us; the launch traced here: 317 us
  matrix products  104 us (32%)
  starting transfers between devices  84.4 us (26%)
  waiting for transfers between devices  60.1 us (19%)
  other arithmetic  51 us (16%)
  local copies, waits for them, and re-layouts  15 us (5%)
    ppermute x8, starting transfers between devices, device_step(): lax.ppermute(kv_first, 'cp', [(sender, sender + offset) for sender in ran...  67.2 us
    ppermute x8, waiting for transfers between devices, device_step(): lax.ppermute(kv_second, 'cp', [(sender, sender - offset) for sender in ra...  47.7 us
    dot_general x4, matrix products, one_block(): jnp.einsum('nkgqs,nskd->nqkgd', exp_scores.astype(jnp.bfloat16), v_part,...  40.8 us
    reduce_sum x4, other arithmetic, one_block(): row_sum = jnp.sum(exp_scores, axis=-1)  36 us
    dot_general x4, matrix products, one_block(): jnp.einsum('nqkgd,nskd->nkgqs', q_part, k_part, preferred_element_type=jn...  35.7 us
    ppermute x8, starting transfers between devices, device_step(): lax.ppermute(kv_second, 'cp', [(sender, sender - offset) for sender in ra...  12.5 us
    ppermute x8, waiting for transfers between devices, device_step(): lax.ppermute(kv_first, 'cp', [(sender, sender + offset) for sender in ran...  12.3 us
    dot_general x1, matrix products, device_step(): jnp.einsum('nqd,dhe->nqhe', x_halves, w_q, preferred_element_type=jnp.flo...  9.09 us
  transfers between devices with their start and end apart: 23, of which 8 were waited for; matrix products, arithmetic and copies ran while one was open for 6% of the time, Pallas kernels for 0%

commit v1 on v0

v1 whole, which is shorter than its diff:
```python
import functools

import jax
import jax.numpy as jnp
from jax import lax
from jax.experimental import pallas as pl
from jax.experimental.pallas import tpu as pltpu
from jax.sharding import PartitionSpec as P

WINDOW = 4096
ROPE_BASE = 10000.0
LOG2E = 1.4426950408889634
NEG = -jnp.inf
RB = 256
CORES = 2


def rope_tables(positions, head_dim):
    half_dim = head_dim // 2
    inv_freq = 1.0 / (ROPE_BASE ** (jnp.arange(half_dim, dtype=jnp.float32) * (2.0 / head_dim)))
    angles = positions.astype(jnp.float32)[:, None] * inv_freq
    cos_part = jnp.cos(angles)
    sin_part = jnp.sin(angles)
    return jnp.concatenate([cos_part, cos_part], axis=-1), jnp.concatenate([-sin_part, sin_part], axis=-1)


def rotate(values, cos_part, sin_part):
    return values * cos_part + pltpu.roll(values, values.shape[1] // 2, 1) * sin_part


def flash_block(q, keys, vals, masks, state):
    lanes = q.shape[1]
    tiles = []
    for k_t, mask in zip(keys, masks):
        scores = jnp.dot(q, k_t, preferred_element_type=jnp.float32)
        if mask is not None:
            scores = jnp.where(mask, scores, NEG)
        tiles.append([scores[:, j:j + lanes] for j in range(0, scores.shape[1], lanes)])
    flat = [tile for group in tiles for tile in group]
    peak = functools.reduce(jnp.maximum, flat)
    peak = jnp.broadcast_to(jnp.max(peak, axis=1, keepdims=True), peak.shape)
    if state is not None:
        peak = jnp.maximum(state[0], peak)
    probs = [[jnp.exp2((tile - peak) * LOG2E) for tile in group] for group in tiles]
    total = functools.reduce(jnp.add, [tile for group in probs for tile in group])
    out = None
    for group, v in zip(probs, vals):
        p = jnp.concatenate([tile.astype(jnp.bfloat16) for tile in group], axis=1)
        part = jnp.dot(p, v, preferred_element_type=jnp.float32)
        out = part if out is None else out + part
    if state is not None:
        scale = jnp.exp2((state[0] - peak) * LOG2E)
        total = state[1] * scale + total
        out = state[2] * scale + out
    return peak, total, out


def make_attend(q_s, m_s, l_s, acc_s, kbuf, vbuf, heads, chunk):
    blocks = chunk // RB

    def load_state(n, rows):
        return m_s[n, rows, :], l_s[n, rows, :], acc_s[n, rows, :]

    def store_state(n, rows, state):
        m_s[n, rows, :], l_s[n, rows, :], acc_s[n, rows, :] = state

    def full(n, slots, unroll=2):
        def body(step, _):
            for u in range(unroll):
                rows = pl.ds(pl.multiple_of((step * unroll + u) * RB, RB), RB)
                state = flash_block(q_s[n, rows, :], [kbuf[s] for s in slots], [vbuf[s] for s in slots], [None] * len(slots), load_state(n, rows))
                store_state(n, rows, state)
            return 0
        lax.fori_loop(0, heads * blocks // unroll, body, 0)

    def masked(n, slot, diag):
        row_ids = lax.broadcasted_iota(jnp.int32, (RB, RB), 0)
        col_ids = lax.broadcasted_iota(jnp.int32, (RB, RB), 1)
        tri = (col_ids <= row_ids) if diag else (col_ids > row_ids)

        def body(h, _):
            for tb in range(blocks):
                rows = pl.ds(pl.multiple_of(h * chunk + tb * RB, RB), RB)
                whole = range(0, tb) if diag else range(tb + 1, blocks)
                picks = [(kb, None) for kb in whole] + [(tb, tri)]
                keys = [kbuf[slot, :, kb * RB:(kb + 1) * RB] for kb, _ in picks]
                vals = [vbuf[slot, kb * RB:(kb + 1) * RB, :] for kb, _ in picks]
                state = flash_block(q_s[n, rows, :], keys, vals, [m for _, m in picks], None if diag else load_state(n, rows))
                store_state(n, rows, state)
            return 0
        lax.fori_loop(0, heads, body, 0)

    return full, masked


def fused_kernel(cp_size, rounds, heads, cos_ref, sin_ref, x_hbm, wk_hbm, wv_hbm, wq_hbm, o_ref,
                 xbuf, wkv, wq_raw, wq_f32, wq, q_s, m_s, l_s, acc_s, kbuf, vbuf,
                 x_sem, w_sem, rail_send_sem, rail_recv_sem, sib_send_sem, sib_recv_sem):
    head_dim = q_s.shape[2]
    chunk = vbuf.shape[1]
    chips = cp_size // CORES
    me = lax.axis_index('cp')
    c = me // CORES
    b = me % CORES
    is_last = c == chips - 1
    above, below, sibling = me + CORES, me - CORES, c * CORES + (1 - b)
    has_above, has_below = c < chips - 1, c > 0

    def slot(n, r, s):
        return (n * (rounds + 1) + r) * 2 + s

    wk_copy = pltpu.make_async_copy(wk_hbm, wkv.at[:, :head_dim], w_sem.at[0])
    wv_copy = pltpu.make_async_copy(wv_hbm, wkv.at[:, head_dim:], w_sem.at[1])
    wq_copy = pltpu.make_async_copy(wq_hbm, wq_raw, w_sem.at[2])
    tiles = x_hbm.shape[0] // RB
    x_copies = [pltpu.make_async_copy(x_hbm.at[pl.ds(t * RB, RB)], xbuf.at[pl.ds(t * RB, RB)], x_sem.at[t]) for t in range(tiles)]
    wk_copy.start()
    wv_copy.start()
    for copy in x_copies:
        copy.start()
    wq_copy.start()

    barrier = pltpu.get_barrier_semaphore()
    pl.semaphore_signal(barrier, inc=1, device_id={'cp': sibling}, device_id_type=pl.DeviceIdType.MESH)

    @pl.when(has_above)
    def _():
        pl.semaphore_signal(barrier, inc=1, device_id={'cp': above}, device_id_type=pl.DeviceIdType.MESH)

    @pl.when(has_below)
    def _():
        pl.semaphore_signal(barrier, inc=1, device_id={'cp': below}, device_id_type=pl.DeviceIdType.MESH)

    bufs = (kbuf, vbuf)

    def rail(n, r, kv):
        if n == 0:
            src, cond, target = slot(0, r - 1, 0), has_above & (c >= r - 1), above
        else:
            src = slot(1, 0, 0) if r == 1 else jnp.where(is_last, slot(0, r - 2, 0), slot(1, r - 1, 0))
            cond, target = has_below, below
        return cond, pltpu.make_async_remote_copy(
            src_ref=bufs[kv].at[src], dst_ref=bufs[kv].at[slot(n, r, 0)],
            send_sem=rail_send_sem.at[n, r - 1, kv], recv_sem=rail_recv_sem.at[n, r - 1, kv],
            device_id={'cp': target}, device_id_type=pl.DeviceIdType.MESH)

    def arrives(n, r):
        return c >= r if n == 0 else has_above

    def sib(n, r, kv):
        return pltpu.make_async_remote_copy(
            src_ref=bufs[kv].at[slot(n, r, 0)], dst_ref=bufs[kv].at[slot(n, r, 1)],
            send_sem=sib_send_sem.at[n, r, kv], recv_sem=sib_recv_sem.at[n, r, kv],
            device_id={'cp': sibling}, device_id_type=pl.DeviceIdType.MESH)

    own_push = ((b == 0) | is_last, b == 1)
    own_take = ((b == 1) | is_last, b == 0)

    def start_rail(n, r, kv):
        cond, copy = rail(n, r, kv)
        pl.when(cond)(copy.start)

    def relay(n, r, kv):
        @pl.when(arrives(n, r))
        def _():
            rail(n, r, kv)[1].wait_recv()
            sib(n, r, kv).start()
        if r < rounds:
            start_rail(n, r + 1, kv)

    def take_sib(n, r):
        cond = own_take[n] if r == 0 else arrives(n, r)

        @pl.when(cond)
        def _():
            for kv in range(2):
                sib(n, r, kv).wait_recv()

    full, masked = make_attend(q_s, m_s, l_s, acc_s, kbuf, vbuf, heads, chunk)

    def project_kv(n):
        for tb in range(chunk // RB):
            t = n * (chunk // RB) + tb
            x_copies[t].wait()
            rows = pl.ds(t * RB, RB)
            kv = jnp.dot(xbuf[rows, :], wkv[...], preferred_element_type=jnp.float32).astype(jnp.bfloat16)
            k = rotate(kv[:, :head_dim].astype(jnp.float32), cos_ref[rows, :], sin_ref[rows, :])
            kbuf[slot(n, 0, 0), :, tb * RB:(tb + 1) * RB] = k.T.astype(jnp.bfloat16)
            vbuf[slot(n, 0, 0), tb * RB:(tb + 1) * RB, :] = kv[:, head_dim:]

    wk_copy.wait()
    wv_copy.wait()
    project_kv(0)
    pl.semaphore_wait(barrier, 1 + has_above.astype(jnp.int32) + has_below.astype(jnp.int32))
    for n in range(2):
        if n == 1:
            project_kv(1)
        for kv in range(2):
            start_rail(n, 1, kv)
        @pl.when(own_push[n])
        def _(n=n):
            for kv in range(2):
                sib(n, 0, kv).start()

    wq_copy.wait()
    depth = wq.shape[0]
    span = wq_f32.shape[0] // heads

    def unpack(step, _):
        wq_f32[...] = wq_raw[pl.ds(pl.multiple_of(step * span * heads, span * heads), span * heads), :].astype(jnp.float32)
        for h in range(heads):
            wq[pl.ds(pl.multiple_of(step * span, span), span), h * head_dim:(h + 1) * head_dim] = wq_f32[pl.ds(h, span, stride=heads), :].astype(jnp.bfloat16)
        return 0
    lax.fori_loop(0, depth // span, unpack, 0)

    def project_q(t, _):
        rows = pl.ds(pl.multiple_of(t * RB, RB), RB)
        n = t // (chunk // RB)
        tb = t % (chunk // RB)
        for h in range(heads):
            qh = jnp.dot(xbuf[rows, :], wq[:, h * head_dim:(h + 1) * head_dim], preferred_element_type=jnp.float32).astype(jnp.bfloat16).astype(jnp.float32)
            qh = rotate(qh, cos_ref[rows, :], sin_ref[rows, :]) * (head_dim ** -0.5)
            q_s[n, pl.ds(pl.multiple_of(h * chunk + tb * RB, RB), RB), :] = qh.astype(jnp.bfloat16)
        return 0
    lax.fori_loop(0, tiles, project_q, 0)

    masked(0, slot(0, 0, 0), True)
    masked(1, slot(1, 0, 0), True)
    take_sib(0, 0)
    take_sib(1, 0)

    @pl.when(b == 1)
    def _():
        full(0, [slot(0, 0, 1)])

    @pl.when(b == 0)
    def _():
        full(1, [slot(1, 0, 1)])

    def pair(n, r):
        take_sib(n, r)
        if n == 0:
            @pl.when(c >= r)
            def _():
                full(0, [slot(0, r, 0), slot(0, r, 1)])
        else:
            full(1, [jnp.where(is_last, slot(0, r - 1, s), slot(1, r, s)) for s in range(2)])

    def edge(n):
        r = rounds
        take_sib(n, r)
        if n == 0:
            @pl.when(c >= r)
            def _():
                masked(0, slot(0, r, 0), False)

                @pl.when(b == 0)
                def _():
                    full(0, [slot(0, r, 1)])
        else:
            flip = (c > chips - 1 - r).astype(jnp.int32)
            base = jnp.where(is_last, slot(0, r - 1, 0), slot(1, r, 0))
            masked(1, base + flip, False)

            @pl.when(b == 1)
            def _():
                full(1, [base + 1 - flip])

    for r in range(1, rounds + 1):
        relay(0, r, 0)
        relay(1, r, 0)
        if r > 1:
            pair(0, r - 1)
        relay(0, r, 1)
        relay(1, r, 1)
        if r > 1:
            pair(1, r - 1)
    for n in range(2):
        edge(n)

    def finish(h, _):
        for n in range(2):
            rows = pl.ds(pl.multiple_of(h * chunk, chunk), chunk)
            total = jnp.sum(l_s[n, rows, :], axis=1, keepdims=True)
            o_ref[n * chunk:(n + 1) * chunk, pl.ds(pl.multiple_of(h * head_dim, head_dim), head_dim)] = (acc_s[n, rows, :] / total).astype(jnp.bfloat16)
        return 0
    lax.fori_loop(0, heads, finish, 0)

    for n in range(2):
        for kv in range(2):
            for r in range(1, rounds + 1):
                cond, copy = rail(n, r, kv)
                pl.when(cond)(copy.wait_send)
                pl.when(arrives(n, r))(sib(n, r, kv).wait_send)
            pl.when(own_push[n])(sib(n, 0, kv).wait_send)


def out_kernel(o_ref, w_ref, y_ref):
    y_ref[...] = jnp.dot(o_ref[...], w_ref[...], preferred_element_type=jnp.float32).astype(jnp.bfloat16)


def solution(mesh):
    cp_size = mesh.shape['cp']

    def device_step(hidden, w_q, w_k, w_v, w_o):
        rows, model_dim = hidden.shape
        chunk = rows // 2
        heads, head_dim = w_q.shape[1], w_q.shape[2]
        rounds = WINDOW // chunk // 2
        me = lax.axis_index('cp')
        chunk_ids = jnp.stack([me, 2 * cp_size - 1 - me])
        positions = (chunk_ids[:, None] * chunk + jnp.arange(chunk)[None, :]).reshape(rows)
        cos_part, sin_part = rope_tables(positions, head_dim)
        slots = 2 * (rounds + 1) * 2
        vmem = pl.BlockSpec(memory_space=pltpu.VMEM)
        hbm = pl.BlockSpec(memory_space=pl.ANY)
        attended = pl.pallas_call(
            functools.partial(fused_kernel, cp_size, rounds, heads),
            out_shape=jax.ShapeDtypeStruct((rows, heads * head_dim), jnp.bfloat16),
            in_specs=[vmem, vmem, hbm, hbm, hbm, hbm],
            out_specs=vmem,
            scratch_shapes=[
                pltpu.VMEM((rows, model_dim), jnp.bfloat16),
                pltpu.VMEM((model_dim, 2 * head_dim), jnp.bfloat16),
                pltpu.VMEM((model_dim * heads, head_dim), jnp.bfloat16),
                pltpu.VMEM((512 * heads, head_dim), jnp.float32),
                pltpu.VMEM((model_dim, heads * head_dim), jnp.bfloat16),
                pltpu.VMEM((2, heads * chunk, head_dim), jnp.bfloat16),
                pltpu.VMEM((2, heads * chunk, head_dim), jnp.float32),
                pltpu.VMEM((2, heads * chunk, head_dim), jnp.float32),
                pltpu.VMEM((2, heads * chunk, head_dim), jnp.float32),
                pltpu.VMEM((slots, head_dim, chunk), jnp.bfloat16),
                pltpu.VMEM((slots, chunk, head_dim), jnp.bfloat16),
                pltpu.SemaphoreType.DMA((rows // RB,)),
                pltpu.SemaphoreType.DMA((3,)),
                pltpu.SemaphoreType.DMA((2, rounds, 2)),
                pltpu.SemaphoreType.DMA((2, rounds, 2)),
                pltpu.SemaphoreType.DMA((2, rounds + 1, 2)),
                pltpu.SemaphoreType.DMA((2, rounds + 1, 2)),
            ],
            compiler_params=pltpu.CompilerParams(collective_id=0, has_side_effects=True, vmem_limit_bytes=60 << 20),
        )(cos_part, sin_part, hidden, w_k.reshape(model_dim, head_dim), w_v.reshape(model_dim, head_dim), w_q.reshape(model_dim * heads, head_dim))
        width = 512
        return pl.pallas_call(
            out_kernel,
            out_shape=jax.ShapeDtypeStruct((rows, model_dim), jnp.bfloat16),
            grid=(model_dim // width,),
            in_specs=[pl.BlockSpec((rows, heads * head_dim), lambda j: (0, 0)), pl.BlockSpec((heads * head_dim, width), lambda j: (0, j))],
            out_specs=pl.BlockSpec((rows, width), lambda j: (0, j)),
        )(attended, w_o.reshape(heads * head_dim, model_dim))

    return jax.shard_map(device_step, mesh=mesh, in_specs=(P(('dp', 'cp'), None), P(), P(), P(), P()), out_specs=P(('dp', 'cp'), None), check_vma=False)
```

time: 320 us -> 87.5 us (0.27)
  the two profiles are of different devices: /device:TPU:55 before, /device:TPU:180 now
where the time goes in v1:
time: 87.5 us; the launch traced here: 87.2 us
  Pallas kernels  83.8 us (96%)
  other arithmetic  3.39 us (4%)
    pallas_call x1, Pallas kernels, device_step(): pl.pallas_call(functools.partial(fused_kernel, cp_size, rounds, heads), o...  73.5 us
    pallas_call x1, Pallas kernels, device_step(): pl.pallas_call(out_kernel, out_shape=jax.ShapeDtypeStruct((rows, model_di...  10.3 us
    neg x1, other arithmetic, rope_tables(): -sin_part  1.9 us

profile of v1, /device:TPU:180, one launch (start us, length us, event | category | flops | bytes accessed | tf_op | source)
XLA Modules:
  0.0 87.2 jit_solution(2096169662030912350)
XLA Ops:
  0.0 0.1 add_multiply_fusion
  0.1 0.1 convert_bitcast_fusion
  0.2 1.9 %fusion = (f32[1024,64]{1,0:T(8,128)S(1)}, f32[1024,64]{1,0:T(8,128)S(1)}, f32[1024,64]{1,0:T(8,128)S(1)}) fusion(f32[64]{0:T(128)S(1)} %negate_power_fusion, f32[1024]{0:T(1024)S(1)} %bitcast.13), kind=kLoop, calls=%fused_computation.4 | loop fusion | flops 131072 | bytes 790784 | tf_op jit(solution)/shard_map/neg | solution.py:24
  2.1 1.3 %pad_maximum_fusion = (f32[1024,128]{1,0:T(8,128)}, f32[1024,128]{1,0:T(8,128)}) fusion(f32[1024,64]{1,0:T(8,128)S(1)} %get-tuple-element.7, f32[1024,64]{1,0:T(8,128)S(1)} %get-tuple-element.6, f32[1024,64]{1,0:T(8,128)S(1)} %get-tuple-element.5), kind=kLoop, calls=%fused_computation.2 | loop fusion | flops 262144 | bytes 1835008 | tf_op jit(solution)/shard_map/concatenate | solution.py:24
  3.4 73.5 %shard_map.55.o_ref = bf16[1024,512]{1,0:T(8,128)(2,1)} custom-call(f32[1024,128]{1,0:T(8,128)} %get-tuple-element.8.cos_ref, f32[1024,128]{1,0:T(8,128)} %get-tuple-element.9.sin_ref, bf16[1024,4096]{1,0:T(8,128)(2,1)} %x_hbm.1, bf16[4096,128]{1,0:T(8,128)(2,1)} %bitcast.11, bf16[4096,128]{1,0:T(8,128)(2,1)} %bitcast.12, bf16[16384,128]{1,0:T(8,128)(2,1)} %bitcast.10), custom_call_target="tpu_custom_call" | custom-call | tf_op jit(solution)/shard_map/pallas_call | solution.py:317
  76.9 10.3 %shard_map.56 = bf16[1024,4096]{1,0:T(8,128)(2,1)} custom-call(bf16[1024,512]{1,0:T(8,128)(2,1)} %shard_map.55.o_ref, bf16[512,4096]{1,0:T(8,128)(2,1)} %bitcast.9), custom_call_target="tpu_custom_call" | custom-call | tf_op jit(solution)/shard_map/pallas_call | solution.py:344
  (2 shorter events, 0.0 us)

commit v2 on v1

v2 whole, which is shorter than its diff:
```python
import functools

import jax
import jax.numpy as jnp
from jax import lax
from jax.experimental import pallas as pl
from jax.experimental.pallas import tpu as pltpu
from jax.sharding import PartitionSpec as P

WINDOW = 4096
ROPE_BASE = 10000.0
LOG2E = 1.4426950408889634
RB = 256
SUB = 8
CORES = 2


def rope_tables(positions, head_dim):
    half_dim = head_dim // 2
    inv_freq = 1.0 / (ROPE_BASE ** (jnp.arange(half_dim, dtype=jnp.float32) * (2.0 / head_dim)))
    angles = positions.astype(jnp.float32)[:, None] * inv_freq
    cos_part = jnp.cos(angles)
    sin_part = jnp.sin(angles)
    return jnp.concatenate([cos_part, cos_part], axis=-1), jnp.concatenate([-sin_part, sin_part], axis=-1)


def rotate(values, cos_part, sin_part):
    return values * cos_part + pltpu.roll(values, values.shape[1] // 2, 1) * sin_part


def score_part(q, keys, mask, s_ref, row, peak):
    scores = jnp.dot(keys, q, preferred_element_type=jnp.float32)
    if mask is not None:
        scores = jnp.where(mask, scores, -jnp.inf)
    rows = scores.shape[0]
    s_ref[row:row + rows, :] = scores
    top = jnp.max(scores.reshape(rows // SUB, SUB, RB), axis=0)
    return top if peak is None else jnp.maximum(peak, top)


def value_part(s_ref, row, vals, peak, total):
    rows = vals.shape[1]
    probs = jnp.exp2((s_ref[row:row + rows, :].reshape(rows // SUB, SUB, RB) - peak[None]) * LOG2E)
    total = total + jnp.sum(probs, axis=0)
    out = jnp.dot(vals, probs.reshape(rows, RB).astype(jnp.bfloat16), preferred_element_type=jnp.float32)
    return total, out


class Step:
    def __init__(self, node, full=(), diag=None, edge=None):
        self.node, self.full, self.diag, self.edge = node, full, diag, edge

    def parts(self, tb, blocks):
        found = []
        size = blocks * RB
        if self.diag is not None:
            if tb:
                found.append((self.diag, 0, tb * RB, None))
            found.append((self.diag, tb * RB, (tb + 1) * RB, 'le'))
        if self.edge is not None:
            found.append((self.edge, tb * RB, (tb + 1) * RB, 'gt'))
            if tb + 1 < blocks:
                found.append((self.edge, (tb + 1) * RB, size, None))
        for s in self.full:
            found.append((s, 0, size, None))
        return found


def fused_kernel(cp_size, rounds, heads, cos_ref, sin_ref, x_hbm, wk_hbm, wv_hbm, wq_hbm, o_ref,
                 xbuf, wkv, wq_raw, wq_f32, wq, q_s, m_s, l_s, acc_s, kbuf, vbuf,
                 x_sem, w_sem, rail_send_sem, rail_recv_sem, sib_send_sem, sib_recv_sem, *score_refs):
    head_dim = q_s.shape[1]
    chunk = kbuf.shape[1]
    blocks = chunk // RB
    count = heads * blocks
    chips = cp_size // CORES
    me = lax.axis_index('cp')
    c = me // CORES
    b = me % CORES
    is_last = c == chips - 1
    above, below, sibling = me + CORES, me - CORES, c * CORES + (1 - b)
    has_above, has_below = c < chips - 1, c > 0
    s_refs = (score_refs[:count], score_refs[count:2 * count])
    x_refs = (score_refs[2 * count:3 * count], score_refs[3 * count:])

    def slot(n, r, s):
        return (n * (rounds + 1) + r) * 2 + s

    wk_copy = pltpu.make_async_copy(wk_hbm, wkv.at[:, :head_dim], w_sem.at[0])
    wv_copy = pltpu.make_async_copy(wv_hbm, wkv.at[:, head_dim:], w_sem.at[1])
    wq_copy = pltpu.make_async_copy(wq_hbm, wq_raw, w_sem.at[2])
    tiles = x_hbm.shape[0] // RB
    x_copies = [pltpu.make_async_copy(x_hbm.at[pl.ds(t * RB, RB)], xbuf.at[pl.ds(t * RB, RB)], x_sem.at[t]) for t in range(tiles)]
    wk_copy.start()
    wv_copy.start()
    for copy in x_copies:
        copy.start()
    wq_copy.start()

    m_s[...] = jnp.full_like(m_s, -jnp.inf)
    l_s[...] = jnp.zeros_like(l_s)
    acc_s[...] = jnp.zeros_like(acc_s)

    barrier = pltpu.get_barrier_semaphore()
    pl.semaphore_signal(barrier, inc=1, device_id={'cp': sibling}, device_id_type=pl.DeviceIdType.MESH)

    @pl.when(has_above)
    def _():
        pl.semaphore_signal(barrier, inc=1, device_id={'cp': above}, device_id_type=pl.DeviceIdType.MESH)

    @pl.when(has_below)
    def _():
        pl.semaphore_signal(barrier, inc=1, device_id={'cp': below}, device_id_type=pl.DeviceIdType.MESH)

    bufs = (kbuf, vbuf)

    def rail(n, r, kv):
        if n == 0:
            src, cond, target = slot(0, r - 1, 0), has_above & (c >= r - 1), above
        else:
            src = slot(1, 0, 0) if r == 1 else jnp.where(is_last, slot(0, r - 2, 0), slot(1, r - 1, 0))
            cond, target = has_below, below
        return cond, pltpu.make_async_remote_copy(
            src_ref=bufs[kv].at[src], dst_ref=bufs[kv].at[slot(n, r, 0)],
            send_sem=rail_send_sem.at[n, r - 1, kv], recv_sem=rail_recv_sem.at[n, r - 1, kv],
            device_id={'cp': target}, device_id_type=pl.DeviceIdType.MESH)

    def arrives(n, r):
        return c >= r if n == 0 else has_above

    def sib(n, r, kv):
        return pltpu.make_async_remote_copy(
            src_ref=bufs[kv].at[slot(n, r, 0)], dst_ref=bufs[kv].at[slot(n, r, 1)],
            send_sem=sib_send_sem.at[n, r, kv], recv_sem=sib_recv_sem.at[n, r, kv],
            device_id={'cp': sibling}, device_id_type=pl.DeviceIdType.MESH)

    own_push = ((b == 0) | is_last, b == 1)
    own_take = ((b == 1) | is_last, b == 0)

    def start_rail(n, r, kv):
        cond, copy = rail(n, r, kv)
        pl.when(cond)(copy.start)

    def relay(n, r, kv):
        @pl.when(arrives(n, r))
        def _():
            rail(n, r, kv)[1].wait_recv()
            sib(n, r, kv).start()
        if r < rounds:
            start_rail(n, r + 1, kv)

    def project_kv(n):
        for tb in range(blocks):
            t = n * blocks + tb
            x_copies[t].wait()
            rows = pl.ds(t * RB, RB)
            kv = jnp.dot(xbuf[rows, :], wkv[...], preferred_element_type=jnp.float32).astype(jnp.bfloat16).astype(jnp.float32)
            k = rotate(kv[:, :head_dim], cos_ref[rows, :], sin_ref[rows, :])
            kbuf[slot(n, 0, 0), tb * RB:(tb + 1) * RB, :] = k.astype(jnp.bfloat16)
            vbuf[slot(n, 0, 0), :, tb * RB:(tb + 1) * RB] = kv[:, head_dim:].T.astype(jnp.bfloat16)

    wk_copy.wait()
    wv_copy.wait()
    project_kv(0)
    pl.semaphore_wait(barrier, 1 + has_above.astype(jnp.int32) + has_below.astype(jnp.int32))
    for n in range(2):
        if n == 1:
            project_kv(1)
        for kv in range(2):
            start_rail(n, 1, kv)

        @pl.when(own_push[n])
        def _(n=n):
            for kv in range(2):
                sib(n, 0, kv).start()

    wq_copy.wait()
    depth = wq.shape[0]
    span = wq_f32.shape[0] // heads

    def unpack(step, _):
        wq_f32[...] = wq_raw[pl.ds(pl.multiple_of(step * span * heads, span * heads), span * heads), :].astype(jnp.float32)
        for h in range(heads):
            wq[pl.ds(pl.multiple_of(step * span, span), span), h * head_dim:(h + 1) * head_dim] = wq_f32[pl.ds(h, span, stride=heads), :].astype(jnp.bfloat16)
        return 0
    lax.fori_loop(0, depth // span, unpack, 0)

    def project_q(t, _):
        rows = pl.ds(pl.multiple_of(t * RB, RB), RB)
        n = t // blocks
        tb = t % blocks
        q = jnp.dot(xbuf[rows, :], wq[...], preferred_element_type=jnp.float32).astype(jnp.bfloat16).astype(jnp.float32)
        for h in range(heads):
            qh = rotate(q[:, h * head_dim:(h + 1) * head_dim], cos_ref[rows, :], sin_ref[rows, :]) * (head_dim ** -0.5)
            q_s[n, :, pl.ds(pl.multiple_of(h * chunk + tb * RB, RB), RB)] = qh.T.astype(jnp.bfloat16)
        return 0
    lax.fori_loop(0, tiles, project_q, 0)

    key_ids = lax.broadcasted_iota(jnp.int32, (RB, RB), 0)
    query_ids = lax.broadcasted_iota(jnp.int32, (RB, RB), 1)

    def mask_of(kind):
        return None if kind is None else (key_ids <= query_ids if kind == 'le' else key_ids > query_ids)

    def region(values, scores, parity):
        for i in range(count):
            cols = slice(i * RB, (i + 1) * RB)
            s_parts = scores.parts(i % blocks, blocks) if scores is not None else []
            v_parts = values.parts(i % blocks, blocks) if values is not None else []
            if values is not None:
                n = values.node
                m_old = m_s[n, :, cols]
                peak = jnp.maximum(m_old, jnp.broadcast_to(jnp.max(x_refs[parity][i][...], axis=0, keepdims=True), m_old.shape))
                scale = jnp.exp2((m_old - peak) * LOG2E)
                total = l_s[n, :, cols] * scale
            out = top = None
            s_row = v_row = 0
            for j in range(max(len(s_parts), len(v_parts))):
                if j < len(s_parts):
                    at, lo, hi, kind = s_parts[j]
                    top = score_part(q_s[scores.node, :, cols], kbuf[at, lo:hi, :], mask_of(kind), s_refs[1 - parity][i], s_row, top)
                    s_row += hi - lo
                if j < len(v_parts):
                    at, lo, hi, kind = v_parts[j]
                    total, part = value_part(s_refs[parity][i], v_row, vbuf[at, :, lo:hi], peak, total)
                    out = part if out is None else out + part
                    v_row += hi - lo
            if scores is not None:
                x_refs[1 - parity][i][...] = top
            if values is not None:
                m_s[n, :, cols] = peak
                l_s[n, :, cols] = total
                acc_s[n, :, cols] = (acc_s[n, :, cols].reshape(head_dim // SUB, SUB, RB) * scale[None]).reshape(head_dim, RB) + out

    def pair_slots(n, r):
        if n == 0:
            return [slot(0, r, s) for s in range(2)]
        return [jnp.where(is_last, slot(0, r - 1, s), slot(1, r, s)) for s in range(2)]

    one_n, two_n = 1 - b, b
    flip = (c > chips - 1 - rounds).astype(jnp.int32)
    high = jnp.where(is_last, slot(0, rounds - 1, 0), slot(1, rounds, 0))
    low = slot(0, rounds, 0)

    def edge_slots(node):
        return jnp.where(node == 0, low, high + flip), jnp.where(node == 0, low + 1, high + 1 - flip)

    def reaches(node):
        return (node == 1) | (c >= rounds)

    always = me != cp_size
    steps = [
        (Step(two_n, diag=slot(0, 0, 0) + two_n * slot(1, 0, 0)), always),
        (Step(one_n, diag=slot(0, 0, 0) + one_n * slot(1, 0, 0), full=[slot(0, 0, 1) + one_n * slot(1, 0, 0)]), always),
    ]
    for r in range(1, rounds):
        for n in range(2):
            steps.append((Step(n, full=pair_slots(n, r)), (c >= r) if n == 0 else always))
    near, far = edge_slots(two_n), edge_slots(one_n)
    steps.append((Step(two_n, edge=near[0], full=[near[1]]), reaches(two_n)))
    steps.append((Step(one_n, edge=far[0]), reaches(one_n)))

    def relay_both(r, kv):
        for n in range(2):
            relay(n, r, kv)

    def take(n, r, kv):
        cond = own_take[n] if r == 0 else arrives(n, r)
        pl.when(cond)(sib(n, r, kv).wait_recv)

    before = [[] for _ in steps]
    before[0] += [('relay', 1, 0), ('take', 0, 0, 0), ('take', 1, 0, 0)]
    before[1] += [('relay', 1, 1), ('take', 0, 0, 1), ('take', 1, 0, 1), ('take', 0, 1, 0)]
    for r in range(1, rounds):
        at = 2 * r
        before[at] += [('relay', r + 1, 0), ('take', 0, r, 1), ('take', 1, r, 0)]
        before[at + 1] += [('relay', r + 1, 1), ('take', 1, r, 1), ('take', 0, r + 1, 0)]
    before[2 * rounds - 1] += [('take', 1, rounds, 0)]
    before[2 * rounds] += [('take', 0, rounds, 1), ('take', 1, rounds, 1)]

    region(None, steps[0][0], 1)
    for i, (step, valid) in enumerate(steps):
        for what, *args in before[i]:
            (relay_both if what == 'relay' else take)(*args)
        following = steps[i + 1][0] if i + 1 < len(steps) else None
        pl.when(valid)(functools.partial(region, step, following, i % 2))
        if valid is not always and following is not None:
            pl.when(jnp.logical_not(valid))(functools.partial(region, None, following, i % 2))

    def finish(h, _):
        for n in range(2):
            cols = pl.ds(pl.multiple_of(h * chunk, chunk), chunk)
            total = jnp.sum(l_s[n, :, cols], axis=0, keepdims=True)
            o_ref[n * chunk:(n + 1) * chunk, pl.ds(pl.multiple_of(h * head_dim, head_dim), head_dim)] = (acc_s[n, :, cols] / total).T.astype(jnp.bfloat16)
        return 0
    lax.fori_loop(0, heads, finish, 0)

    for n in range(2):
        for kv in range(2):
            for r in range(1, rounds + 1):
                cond, copy = rail(n, r, kv)
                pl.when(cond)(copy.wait_send)
                pl.when(arrives(n, r))(sib(n, r, kv).wait_send)
            pl.when(own_push[n])(sib(n, 0, kv).wait_send)


def out_kernel(o_ref, w_ref, y_ref):
    y_ref[...] = jnp.dot(o_ref[...], w_ref[...], preferred_element_type=jnp.float32).astype(jnp.bfloat16)


def solution(mesh):
    cp_size = mesh.shape['cp']

    def device_step(hidden, w_q, w_k, w_v, w_o):
        rows, model_dim = hidden.shape
        chunk = rows // 2
        heads, head_dim = w_q.shape[1], w_q.shape[2]
        rounds = WINDOW // chunk // 2
        me = lax.axis_index('cp')
        chunk_ids = jnp.stack([me, 2 * cp_size - 1 - me])
        positions = (chunk_ids[:, None] * chunk + jnp.arange(chunk)[None, :]).reshape(rows)
        cos_part, sin_part = rope_tables(positions, head_dim)
        slots = 2 * (rounds + 1) * 2
        vmem = pl.BlockSpec(memory_space=pltpu.VMEM)
        hbm = pl.BlockSpec(memory_space=pl.ANY)
        attended = pl.pallas_call(
            functools.partial(fused_kernel, cp_size, rounds, heads),
            out_shape=jax.ShapeDtypeStruct((rows, heads * head_dim), jnp.bfloat16),
            in_specs=[vmem, vmem, hbm, hbm, hbm, hbm],
            out_specs=vmem,
            scratch_shapes=[
                pltpu.VMEM((rows, model_dim), jnp.bfloat16),
                pltpu.VMEM((model_dim, 2 * head_dim), jnp.bfloat16),
                pltpu.VMEM((model_dim * heads, head_dim), jnp.bfloat16),
                pltpu.VMEM((512 * heads, head_dim), jnp.float32),
                pltpu.VMEM((model_dim, heads * head_dim), jnp.bfloat16),
                pltpu.VMEM((2, head_dim, heads * chunk), jnp.bfloat16),
                pltpu.VMEM((2, SUB, heads * chunk), jnp.float32),
                pltpu.VMEM((2, SUB, heads * chunk), jnp.float32),
                pltpu.VMEM((2, head_dim, heads * chunk), jnp.float32),
                pltpu.VMEM((slots, chunk, head_dim), jnp.bfloat16),
                pltpu.VMEM((slots, head_dim, chunk), jnp.bfloat16),
                pltpu.SemaphoreType.DMA((rows // RB,)),
                pltpu.SemaphoreType.DMA((3,)),
                pltpu.SemaphoreType.DMA((2, rounds, 2)),
                pltpu.SemaphoreType.DMA((2, rounds, 2)),
                pltpu.SemaphoreType.DMA((2, rounds + 1, 2)),
                pltpu.SemaphoreType.DMA((2, rounds + 1, 2)),
            ] + [pltpu.VMEM((2 * chunk, RB), jnp.float32)] * (2 * heads * chunk // RB) + [pltpu.VMEM((SUB, RB), jnp.float32)] * (2 * heads * chunk // RB),
            compiler_params=pltpu.CompilerParams(collective_id=0, has_side_effects=True, vmem_limit_bytes=60 << 20),
        )(cos_part, sin_part, hidden, w_k.reshape(model_dim, head_dim), w_v.reshape(model_dim, head_dim), w_q.reshape(model_dim * heads, head_dim))
        band = 256
        return pl.pallas_call(
            out_kernel,
            out_shape=jax.ShapeDtypeStruct((rows, model_dim), jnp.bfloat16),
            grid=(rows // band,),
            in_specs=[pl.BlockSpec((band, heads * head_dim), lambda j: (j, 0)), vmem],
            out_specs=pl.BlockSpec((band, model_dim), lambda j: (j, 0)),
        )(attended, w_o.reshape(heads * head_dim, model_dim))

    return jax.shard_map(device_step, mesh=mesh, in_specs=(P(('dp', 'cp'), None), P(), P(), P(), P()), out_specs=P(('dp', 'cp'), None), check_vma=False)
```

time: 87.5 us -> 56.7 us (0.65)
  the two profiles are of different devices: /device:TPU:180 before, /device:TPU:55 now
where the time goes in v2:
time: 56.7 us; the launch traced here: 56.6 us
  Pallas kernels  53.2 us (94%)
  other arithmetic  3.39 us (6%)
    pallas_call x1, Pallas kernels, device_step(): pl.pallas_call(functools.partial(fused_kernel, cp_size, rounds, heads), o...  44.4 us
    pallas_call x1, Pallas kernels, device_step(): pl.pallas_call(out_kernel, out_shape=jax.ShapeDtypeStruct((rows, model_di...  8.74 us
    neg x1, other arithmetic, rope_tables(): -sin_part  1.9 us
    concatenate x1, other arithmetic, rope_tables(): jnp.concatenate([cos_part, cos_part], axis=-1)  1.32 us

profile of v2, /device:TPU:55, one launch (start us, length us, event | category | flops | bytes accessed | tf_op | source)
XLA Modules:
  0.0 56.6 jit_solution(15647663933999672216)
XLA Ops:
  0.0 0.1 add_multiply_fusion
  0.1 0.1 convert_bitcast_fusion
  0.2 1.9 %fusion = (f32[1024,64]{1,0:T(8,128)S(1)}, f32[1024,64]{1,0:T(8,128)S(1)}, f32[1024,64]{1,0:T(8,128)S(1)}) fusion(f32[64]{0:T(128)S(1)} %negate_power_fusion, f32[1024]{0:T(1024)S(1)} %bitcast.13), kind=kLoop, calls=%fused_computation.4 | loop fusion | flops 131072 | bytes 790784 | tf_op jit(solution)/shard_map/neg | solution.py:24
  2.1 1.3 %pad_maximum_fusion = (f32[1024,128]{1,0:T(8,128)}, f32[1024,128]{1,0:T(8,128)}) fusion(f32[1024,64]{1,0:T(8,128)S(1)} %get-tuple-element.7, f32[1024,64]{1,0:T(8,128)S(1)} %get-tuple-element.6, f32[1024,64]{1,0:T(8,128)S(1)} %get-tuple-element.5), kind=kLoop, calls=%fused_computation.2 | loop fusion | flops 262144 | bytes 1835008 | tf_op jit(solution)/shard_map/concatenate | solution.py:24
  3.4 44.4 %shard_map.55.o_ref = bf16[1024,512]{1,0:T(8,128)(2,1)} custom-call(f32[1024,128]{1,0:T(8,128)} %get-tuple-element.8.cos_ref, f32[1024,128]{1,0:T(8,128)} %get-tuple-element.9.sin_ref, bf16[1024,4096]{1,0:T(8,128)(2,1)} %x_hbm.1, bf16[4096,128]{1,0:T(8,128)(2,1)} %bitcast.11, bf16[4096,128]{1,0:T(8,128)(2,1)} %bitcast.12, bf16[16384,128]{1,0:T(8,128)(2,1)} %bitcast.10), custom_call_target="tpu_custom_call" | custom-call | tf_op jit(solution)/shard_map/pallas_call | solution.py:326
  47.8 8.7 %shard_map.56 = bf16[1024,4096]{1,0:T(8,128)(2,1)} custom-call(bf16[1024,512]{1,0:T(8,128)(2,1)} %shard_map.55.o_ref, bf16[512,4096]{1,0:T(8,128)(2,1)} %bitcast.9), custom_call_target="tpu_custom_call" | custom-call | tf_op jit(solution)/shard_map/pallas_call | solution.py:353
  (2 shorter events, 0.0 us)

commit v3 on v2

--- a/solution.py
+++ b/solution.py
@@ -18,14 +18,14 @@
 def rope_tables(positions, head_dim):
     half_dim = head_dim // 2
     inv_freq = 1.0 / (ROPE_BASE ** (jnp.arange(half_dim, dtype=jnp.float32) * (2.0 / head_dim)))
-    angles = positions.astype(jnp.float32)[:, None] * inv_freq
-    cos_part = jnp.cos(angles)
-    sin_part = jnp.sin(angles)
-    return jnp.concatenate([cos_part, cos_part], axis=-1), jnp.concatenate([-sin_part, sin_part], axis=-1)
+    angles = inv_freq[:, None] * positions.astype(jnp.float32)[None, :]
+    return jnp.cos(angles), jnp.sin(angles)
 
 
 def rotate(values, cos_part, sin_part):
-    return values * cos_part + pltpu.roll(values, values.shape[1] // 2, 1) * sin_part
+    half_dim = values.shape[0] // 2
+    first, second = values[:half_dim], values[half_dim:]
+    return jnp.concatenate([first * cos_part - second * sin_part, second * cos_part + first * sin_part], axis=0)
 
 
 def score_part(q, keys, mask, s_ref, row, peak):
@@ -67,7 +67,7 @@
 
 
 def fused_kernel(cp_size, rounds, heads, cos_ref, sin_ref, x_hbm, wk_hbm, wv_hbm, wq_hbm, o_ref,
-                 xbuf, wkv, wq_raw, wq_f32, wq, q_s, m_s, l_s, acc_s, kbuf, vbuf,
+                 xbuf, wk, wv, wq_raw, wq_f32, wq, q_s, m_s, l_s, acc_s, kbuf, vbuf,
                  x_sem, w_sem, rail_send_sem, rail_recv_sem, sib_send_sem, sib_recv_sem, *score_refs):
     head_dim = q_s.shape[1]
     chunk = kbuf.shape[1]
@@ -86,16 +86,15 @@
     def slot(n, r, s):
         return (n * (rounds + 1) + r) * 2 + s
 
-    wk_copy = pltpu.make_async_copy(wk_hbm, wkv.at[:, :head_dim], w_sem.at[0])
-    wv_copy = pltpu.make_async_copy(wv_hbm, wkv.at[:, head_dim:], w_sem.at[1])
+    wk_copy = pltpu.make_async_copy(wk_hbm, wk, w_sem.at[0])
+    wv_copy = pltpu.make_async_copy(wv_hbm, wv, w_sem.at[1])
     wq_copy = pltpu.make_async_copy(wq_hbm, wq_raw, w_sem.at[2])
     tiles = x_hbm.shape[0] // RB
     x_copies = [pltpu.make_async_copy(x_hbm.at[pl.ds(t * RB, RB)], xbuf.at[pl.ds(t * RB, RB)], x_sem.at[t]) for t in range(tiles)]
+    x_copies[0].start()
     wk_copy.start()
     wv_copy.start()
-    for copy in x_copies:
-        copy.start()
-    wq_copy.start()
+    x_copies[1].start()
 
     m_s[...] = jnp.full_like(m_s, -jnp.inf)
     l_s[...] = jnp.zeros_like(l_s)
@@ -118,7 +117,8 @@
         if n == 0:
             src, cond, target = slot(0, r - 1, 0), has_above & (c >= r - 1), above
         else:
-            src = slot(1, 0, 0) if r == 1 else jnp.where(is_last, slot(0, r - 2, 0), slot(1, r - 1, 0))
+            first = isinstance(r, int) and r == 1
+            src = slot(1, 0, 0) if first else jnp.where(is_last, slot(0, r - 2, 0), slot(1, r - 1, 0))
             cond, target = has_below, below
         return cond, pltpu.make_async_remote_copy(
             src_ref=bufs[kv].at[src], dst_ref=bufs[kv].at[slot(n, r, 0)],
@@ -146,17 +146,22 @@
         def _():
             rail(n, r, kv)[1].wait_recv()
             sib(n, r, kv).start()
-        if r < rounds:
+        if not isinstance(r, int) or r < rounds:
             start_rail(n, r + 1, kv)
 
     def project_kv(n):
         for tb in range(blocks):
             t = n * blocks + tb
             x_copies[t].wait()
-            rows = pl.ds(t * RB, RB)
-            kv = jnp.dot(xbuf[rows, :], wkv[...], preferred_element_type=jnp.float32).astype(jnp.bfloat16).astype(jnp.float32)
-            k = rotate(kv[:, :head_dim], cos_ref[rows, :], sin_ref[rows, :])
-            kbuf[slot(n, 0, 0), tb * RB:(tb + 1) * RB, :] = k.astype(jnp.bfloat16)
+            if t + 2 < tiles:
+                x_copies[t + 2].start()
+            elif t + 2 == tiles:
+                wq_copy.start()
+            rows = slice(t * RB, (t + 1) * RB)
+            w_kv = jnp.concatenate([wk[...], wv[...]], axis=1)
+            kv = jnp.dot(xbuf[rows, :], w_kv, preferred_element_type=jnp.float32).astype(jnp.bfloat16).astype(jnp.float32)
+            k = rotate(kv[:, :head_dim].T, cos_ref[:, rows], sin_ref[:, rows])
+            kbuf[slot(n, 0, 0), tb * RB:(tb + 1) * RB, :] = k.T.astype(jnp.bfloat16)
             vbuf[slot(n, 0, 0), :, tb * RB:(tb + 1) * RB] = kv[:, head_dim:].T.astype(jnp.bfloat16)
 
     wk_copy.wait()
@@ -185,16 +190,13 @@
         return 0
     lax.fori_loop(0, depth // span, unpack, 0)
 
-    def project_q(t, _):
-        rows = pl.ds(pl.multiple_of(t * RB, RB), RB)
-        n = t // blocks
-        tb = t % blocks
+    for t in range(tiles):
+        rows = slice(t * RB, (t + 1) * RB)
+        n, tb = t // blocks, t % blocks
         q = jnp.dot(xbuf[rows, :], wq[...], preferred_element_type=jnp.float32).astype(jnp.bfloat16).astype(jnp.float32)
         for h in range(heads):
-            qh = rotate(q[:, h * head_dim:(h + 1) * head_dim], cos_ref[rows, :], sin_ref[rows, :]) * (head_dim ** -0.5)
-            q_s[n, :, pl.ds(pl.multiple_of(h * chunk + tb * RB, RB), RB)] = qh.T.astype(jnp.bfloat16)
-        return 0
-    lax.fori_loop(0, tiles, project_q, 0)
+            qh = rotate(q[:, h * head_dim:(h + 1) * head_dim].T, cos_ref[:, rows], sin_ref[:, rows]) * (head_dim ** -0.5)
+            q_s[n, :, h * chunk + tb * RB:h * chunk + (tb + 1) * RB] = qh.astype(jnp.bfloat16)
 
     key_ids = lax.broadcasted_iota(jnp.int32, (RB, RB), 0)
     query_ids = lax.broadcasted_iota(jnp.int32, (RB, RB), 1)
@@ -249,43 +251,62 @@
         return (node == 1) | (c >= rounds)
 
     always = me != cp_size
-    steps = [
-        (Step(two_n, diag=slot(0, 0, 0) + two_n * slot(1, 0, 0)), always),
-        (Step(one_n, diag=slot(0, 0, 0) + one_n * slot(1, 0, 0), full=[slot(0, 0, 1) + one_n * slot(1, 0, 0)]), always),
-    ]
-    for r in range(1, rounds):
-        for n in range(2):
-            steps.append((Step(n, full=pair_slots(n, r)), (c >= r) if n == 0 else always))
     near, far = edge_slots(two_n), edge_slots(one_n)
-    steps.append((Step(two_n, edge=near[0], full=[near[1]]), reaches(two_n)))
-    steps.append((Step(one_n, edge=far[0]), reaches(one_n)))
+    own_two = Step(two_n, diag=slot(0, 0, 0) + two_n * slot(1, 0, 0))
+    own_one = Step(one_n, diag=slot(0, 0, 0) + one_n * slot(1, 0, 0), full=[slot(0, 0, 1) + one_n * slot(1, 0, 0)])
+    edge_two = Step(two_n, edge=near[0], full=[near[1]])
+    edge_one = Step(one_n, edge=far[0])
+
+    def pair(n, r):
+        return Step(n, full=pair_slots(n, r))
 
     def relay_both(r, kv):
         for n in range(2):
             relay(n, r, kv)
 
     def take(n, r, kv):
-        cond = own_take[n] if r == 0 else arrives(n, r)
+        cond = own_take[n] if isinstance(r, int) and r == 0 else arrives(n, r)
         pl.when(cond)(sib(n, r, kv).wait_recv)
 
-    before = [[] for _ in steps]
-    before[0] += [('relay', 1, 0), ('take', 0, 0, 0), ('take', 1, 0, 0)]
-    before[1] += [('relay', 1, 1), ('take', 0, 0, 1), ('take', 1, 0, 1), ('take', 0, 1, 0)]
-    for r in range(1, rounds):
-        at = 2 * r
-        before[at] += [('relay', r + 1, 0), ('take', 0, r, 1), ('take', 1, r, 0)]
-        before[at + 1] += [('relay', r + 1, 1), ('take', 1, r, 1), ('take', 0, r + 1, 0)]
-    before[2 * rounds - 1] += [('take', 1, rounds, 0)]
-    before[2 * rounds] += [('take', 0, rounds, 1), ('take', 1, rounds, 1)]
-
-    region(None, steps[0][0], 1)
-    for i, (step, valid) in enumerate(steps):
-        for what, *args in before[i]:
-            (relay_both if what == 'relay' else take)(*args)
-        following = steps[i + 1][0] if i + 1 < len(steps) else None
-        pl.when(valid)(functools.partial(region, step, following, i % 2))
-        if valid is not always and following is not None:
-            pl.when(jnp.logical_not(valid))(functools.partial(region, None, following, i % 2))
+    def run(step, following, parity, valid=None):
+        pl.when(always if valid is None else valid)(functools.partial(region, step, following, parity))
+        if valid is not None and following is not None:
+            pl.when(jnp.logical_not(valid))(functools.partial(region, None, following, parity))
+
+    region(None, own_two, 1)
+    relay_both(1, 0)
+    for n in range(2):
+        take(n, 0, 0)
+    run(own_two, own_one, 0)
+    relay_both(1, 1)
+    for n in range(2):
+        take(n, 0, 1)
+    take(0, 1, 0)
+    run(own_one, pair(0, 1), 1)
+
+    def round_of(r, after_low, after_high):
+        relay_both(r + 1, 0)
+        take(0, r, 1)
+        take(1, r, 0)
+        run(pair(0, r), pair(1, r), 0, c >= r)
+        relay_both(r + 1, 1)
+        take(1, r, 1)
+        after_low()
+        run(pair(1, r), after_high, 1)
+
+    def middle(r, _):
+        round_of(r, lambda: take(0, r + 1, 0), pair(0, r + 1))
+        return 0
+    lax.fori_loop(1, rounds - 1, middle, 0)
+
+    def last_keys():
+        for n in range(2):
+            take(n, rounds, 0)
+    round_of(rounds - 1, last_keys, edge_two)
+    for n in range(2):
+        take(n, rounds, 1)
+    run(edge_two, edge_one, 0, reaches(two_n))
+    run(edge_one, None, 1, reaches(one_n))
 
     def finish(h, _):
         for n in range(2):
@@ -304,8 +325,9 @@
             pl.when(own_push[n])(sib(n, 0, kv).wait_send)
 
 
-def out_kernel(o_ref, w_ref, y_ref):
-    y_ref[...] = jnp.dot(o_ref[...], w_ref[...], preferred_element_type=jnp.float32).astype(jnp.bfloat16)
+def out_kernel(band, o_ref, w_ref, y_ref):
+    rows = pl.ds(pl.multiple_of(pl.program_id(0) * band, band), band)
+    y_ref[...] = jnp.dot(o_ref[rows, :], w_ref[...], preferred_element_type=jnp.float32).astype(jnp.bfloat16)
 
 
 def solution(mesh):
@@ -322,7 +344,7 @@
         cos_part, sin_part = rope_tables(positions, head_dim)
         slots = 2 * (rounds + 1) * 2
         vmem = pl.BlockSpec(memory_space=pltpu.VMEM)
-        hbm = pl.BlockSpec(memory_space=pl.ANY)
+        hbm = pl.BlockSpec(memory_space=pltpu.HBM)
         attended = pl.pallas_call(
             functools.partial(fused_kernel, cp_size, rounds, heads),
             out_shape=jax.ShapeDtypeStruct((rows, heads * head_dim), jnp.bfloat16),
@@ -330,7 +352,8 @@
             out_specs=vmem,
             scratch_shapes=[
                 pltpu.VMEM((rows, model_dim), jnp.bfloat16),
-                pltpu.VMEM((model_dim, 2 * head_dim), jnp.bfloat16),
+                pltpu.VMEM((model_dim, head_dim), jnp.bfloat16),
+                pltpu.VMEM((model_dim, head_dim), jnp.bfloat16),
                 pltpu.VMEM((model_dim * heads, head_dim), jnp.bfloat16),
                 pltpu.VMEM((512 * heads, head_dim), jnp.float32),
                 pltpu.VMEM((model_dim, heads * head_dim), jnp.bfloat16),
@@ -347,15 +370,16 @@
                 pltpu.SemaphoreType.DMA((2, rounds + 1, 2)),
                 pltpu.SemaphoreType.DMA((2, rounds + 1, 2)),
             ] + [pltpu.VMEM((2 * chunk, RB), jnp.float32)] * (2 * heads * chunk // RB) + [pltpu.VMEM((SUB, RB), jnp.float32)] * (2 * heads * chunk // RB),
-            compiler_params=pltpu.CompilerParams(collective_id=0, has_side_effects=True, vmem_limit_bytes=60 << 20),
-        )(cos_part, sin_part, hidden, w_k.reshape(model_dim, head_dim), w_v.reshape(model_dim, head_dim), w_q.reshape(model_dim * heads, head_dim))
+            compiler_params=pltpu.CompilerParams(collective_id=0, has_side_effects=True, vmem_limit_bytes=47 << 20),
+        )(cos_part, sin_part, *(pltpu.with_memory_space_constraint(a, pltpu.HBM) for a in (hidden, w_k.reshape(model_dim, head_dim), w_v.reshape(model_dim, head_dim), w_q.reshape(model_dim * heads, head_dim))))
         band = 256
         return pl.pallas_call(
-            out_kernel,
+            functools.partial(out_kernel, band),
             out_shape=jax.ShapeDtypeStruct((rows, model_dim), jnp.bfloat16),
             grid=(rows // band,),
-            in_specs=[pl.BlockSpec((band, heads * head_dim), lambda j: (j, 0)), vmem],
+            in_specs=[vmem, vmem],
             out_specs=pl.BlockSpec((band, model_dim), lambda j: (j, 0)),
+            compiler_params=pltpu.CompilerParams(vmem_limit_bytes=24 << 20),
         )(attended, w_o.reshape(heads * head_dim, model_dim))
 
     return jax.shard_map(device_step, mesh=mesh, in_specs=(P(('dp', 'cp'), None), P(), P(), P(), P()), out_specs=P(('dp', 'cp'), None), check_vma=False)

time: 56.7 us -> 48.9 us (0.86)
  Pallas kernels: 53.2 us -> 47.7 us
  other arithmetic: 3.39 us -> 1.14 us
    pallas_call x1, Pallas kernels: 44.4 us -> 41.2 us  [device_step(): pl.pallas_call(functools.partial(fused_kernel, cp_size, rounds, heads), o...]
    pallas_call x1, Pallas kernels: 8.74 us -> 6.45 us  [device_step(): pl.pallas_call(functools.partial(out_kernel, band), out_shape=jax.ShapeDt...]
    neg x1 -> x0, other arithmetic: 1.9 us -> none  [rope_tables(): -sin_part]
    concatenate x1 -> x0, other arithmetic: 1.32 us -> none  [rope_tables(): jnp.concatenate([cos_part, cos_part], axis=-1)]
    sin x0 -> x1, other arithmetic: none -> 0.98 us  [rope_tables(): return (jnp.cos(angles), jnp.sin(angles))]
where the time goes in v3:
time: 48.9 us; the launch traced here: 48.8 us
  Pallas kernels  47.7 us (98%)
  other arithmetic  1.14 us (2%)
    pallas_call x1, Pallas kernels, device_step(): pl.pallas_call(functools.partial(fused_kernel, cp_size, rounds, heads), o...  41.2 us
    pallas_call x1, Pallas kernels, device_step(): pl.pallas_call(functools.partial(out_kernel, band), out_shape=jax.ShapeDt...  6.45 us
    sin x1, other arithmetic, rope_tables(): return (jnp.cos(angles), jnp.sin(angles))  0.98 us

profile of v3, /device:TPU:55, one launch (start us, length us, event | category | flops | bytes accessed | tf_op | source)
XLA Modules:
  0.0 48.8 jit_solution(17537475933427526292)
XLA Ops:
  0.0 0.1 add_multiply_fusion
  0.1 0.1 convert_bitcast_fusion
  0.2 0.0 copy-start
  0.2 1.0 %multiply_sine_fusion = (f32[64,1024]{1,0:T(8,128)S(1)}, f32[64,1024]{1,0:T(8,128)S(1)}) fusion(f32[1024]{0:T(1024)S(1)} %bitcast.13, f32[64]{0:T(128)S(1)} %negate_power_fusion), kind=kLoop, calls=%fused_computation | loop fusion | flops 65536 | bytes 528640 | tf_op jit(solution)/shard_map/sin | solution.py:22
  1.2 41.2 %shard_map.55.o_ref = bf16[1024,512]{1,0:T(8,128)(2,1)S(1)} custom-call(f32[64,1024]{1,0:T(8,128)S(1)} %get-tuple-element.6.cos_ref, f32[64,1024]{1,0:T(8,128)S(1)} %get-tuple-element.5.sin_ref, bf16[1024,4096]{1,0:T(8,128)(2,1)} %x_hbm.1, bf16[4096,128]{1,0:T(8,128)(2,1)} %bitcast.11, bf16[4096,128]{1,0:T(8,128)(2,1)} %bitcast.12, bf16[16384,128]{1,0:T(8,128)(2,1)} %bitcast.10), custom_call_target="tpu_custom_call" | custom-call | tf_op jit(solution)/shard_map/pallas_call | solution.py:348
  42.4 0.0 copy-done
  42.4 6.5 %shard_map.56 = bf16[1024,4096]{1,0:T(8,128)(2,1)} custom-call(bf16[1024,512]{1,0:T(8,128)(2,1)S(1)} %shard_map.55.o_ref, bf16[512,4096]{1,0:T(8,128)(2,1)S(1)} %bitcast.9), custom_call_target="tpu_custom_call" | custom-call | tf_op jit(solution)/shard_map/pallas_call | solution.py:376
  (2 shorter events, 0.0 us)
Async XLA Ops:
  0.2 42.2 %copy-start = (bf16[4,128,4096]{2,1,0:T(8,128)(2,1)S(1)}, bf16[4,128,4096]{2,1,0:T(8,128)(2,1)}, u32[]{:S(2)}) copy-start(bf16[4,128,4096]{2,1,0:T(8,128)(2,1)} %param.9) | copy-start | bytes 12582916

commit v4 on v3

--- a/solution.py
+++ b/solution.py
@@ -12,14 +12,14 @@
 LOG2E = 1.4426950408889634
 RB = 256
 SUB = 8
+LANES = 128
 CORES = 2
 
 
-def rope_tables(positions, head_dim):
+def rope_freqs(head_dim):
     half_dim = head_dim // 2
     inv_freq = 1.0 / (ROPE_BASE ** (jnp.arange(half_dim, dtype=jnp.float32) * (2.0 / head_dim)))
-    angles = inv_freq[:, None] * positions.astype(jnp.float32)[None, :]
-    return jnp.cos(angles), jnp.sin(angles)
+    return jnp.broadcast_to(inv_freq[:, None], (half_dim, LANES))
 
 
 def rotate(values, cos_part, sin_part):
@@ -66,8 +66,8 @@
         return found
 
 
-def fused_kernel(cp_size, rounds, heads, cos_ref, sin_ref, x_hbm, wk_hbm, wv_hbm, wq_hbm, o_ref,
-                 xbuf, wk, wv, wq_raw, wq_f32, wq, q_s, m_s, l_s, acc_s, kbuf, vbuf,
+def fused_kernel(cp_size, rounds, heads, freq_ref, x_hbm, wk_hbm, wv_hbm, wq_hbm, wo_hbm, o_ref, wo_ref,
+                 cos_ref, sin_ref, xbuf, wk, wv, wq_raw, wq_f32, wq, q_s, m_s, l_s, acc_s, kbuf, vbuf,
                  x_sem, w_sem, rail_send_sem, rail_recv_sem, sib_send_sem, sib_recv_sem, *score_refs):
     head_dim = q_s.shape[1]
     chunk = kbuf.shape[1]
@@ -89,6 +89,7 @@
     wk_copy = pltpu.make_async_copy(wk_hbm, wk, w_sem.at[0])
     wv_copy = pltpu.make_async_copy(wv_hbm, wv, w_sem.at[1])
     wq_copy = pltpu.make_async_copy(wq_hbm, wq_raw, w_sem.at[2])
+    wo_copy = pltpu.make_async_copy(wo_hbm, wo_ref, w_sem.at[3])
     tiles = x_hbm.shape[0] // RB
     x_copies = [pltpu.make_async_copy(x_hbm.at[pl.ds(t * RB, RB)], xbuf.at[pl.ds(t * RB, RB)], x_sem.at[t]) for t in range(tiles)]
     x_copies[0].start()
@@ -96,10 +97,6 @@
     wv_copy.start()
     x_copies[1].start()
 
-    m_s[...] = jnp.full_like(m_s, -jnp.inf)
-    l_s[...] = jnp.zeros_like(l_s)
-    acc_s[...] = jnp.zeros_like(acc_s)
-
     barrier = pltpu.get_barrier_semaphore()
     pl.semaphore_signal(barrier, inc=1, device_id={'cp': sibling}, device_id_type=pl.DeviceIdType.MESH)
 
@@ -110,6 +107,16 @@
     @pl.when(has_below)
     def _():
         pl.semaphore_signal(barrier, inc=1, device_id={'cp': below}, device_id_type=pl.DeviceIdType.MESH)
+
+    lane_ids = lax.broadcasted_iota(jnp.int32, freq_ref.shape, 1)
+    for n, chunk_id in enumerate((me, 2 * cp_size - 1 - me)):
+        def table(j, _, n=n, chunk_id=chunk_id):
+            angles = freq_ref[...] * (lane_ids + (chunk_id * chunk + j * LANES)).astype(jnp.float32)
+            cols = pl.ds(pl.multiple_of(n * chunk + j * LANES, LANES), LANES)
+            cos_ref[:, cols] = jnp.cos(angles)
+            sin_ref[:, cols] = jnp.sin(angles)
+            return 0
+        lax.fori_loop(0, chunk // LANES, table, 0)
 
     bufs = (kbuf, vbuf)
 
@@ -179,7 +186,12 @@
             for kv in range(2):
                 sib(n, 0, kv).start()
 
+    m_s[...] = jnp.full_like(m_s, -jnp.inf)
+    l_s[...] = jnp.zeros_like(l_s)
+    acc_s[...] = jnp.zeros_like(acc_s)
+
     wq_copy.wait()
+    wo_copy.start()
     depth = wq.shape[0]
     span = wq_f32.shape[0] // heads
 
@@ -284,15 +296,20 @@
     take(0, 1, 0)
     run(own_one, pair(0, 1), 1)
 
-    def round_of(r, after_low, after_high):
+    def round_of(r, after_low, after_high, last=False):
         relay_both(r + 1, 0)
         take(0, r, 1)
         take(1, r, 0)
         run(pair(0, r), pair(1, r), 0, c >= r)
-        relay_both(r + 1, 1)
+        if last:
+            relay(0, r + 1, 1)
+        else:
+            relay_both(r + 1, 1)
         take(1, r, 1)
         after_low()
         run(pair(1, r), after_high, 1)
+        if last:
+            relay(1, r + 1, 1)
 
     def middle(r, _):
         round_of(r, lambda: take(0, r + 1, 0), pair(0, r + 1))
@@ -316,6 +333,7 @@
         return 0
     lax.fori_loop(0, heads, finish, 0)
 
+    wo_copy.wait()
     for n in range(2):
         for kv in range(2):
             for r in range(1, rounds + 1):
@@ -338,19 +356,17 @@
         chunk = rows // 2
         heads, head_dim = w_q.shape[1], w_q.shape[2]
         rounds = WINDOW // chunk // 2
-        me = lax.axis_index('cp')
-        chunk_ids = jnp.stack([me, 2 * cp_size - 1 - me])
-        positions = (chunk_ids[:, None] * chunk + jnp.arange(chunk)[None, :]).reshape(rows)
-        cos_part, sin_part = rope_tables(positions, head_dim)
         slots = 2 * (rounds + 1) * 2
         vmem = pl.BlockSpec(memory_space=pltpu.VMEM)
         hbm = pl.BlockSpec(memory_space=pltpu.HBM)
-        attended = pl.pallas_call(
+        attended, w_out = pl.pallas_call(
             functools.partial(fused_kernel, cp_size, rounds, heads),
-            out_shape=jax.ShapeDtypeStruct((rows, heads * head_dim), jnp.bfloat16),
-            in_specs=[vmem, vmem, hbm, hbm, hbm, hbm],
-            out_specs=vmem,
+            out_shape=[jax.ShapeDtypeStruct((rows, heads * head_dim), jnp.bfloat16), jax.ShapeDtypeStruct((heads * head_dim, model_dim), jnp.bfloat16)],
+            in_specs=[vmem, hbm, hbm, hbm, hbm, hbm],
+            out_specs=[vmem, vmem],
             scratch_shapes=[
+                pltpu.VMEM((head_dim // 2, rows), jnp.float32),
+                pltpu.VMEM((head_dim // 2, rows), jnp.float32),
                 pltpu.VMEM((rows, model_dim), jnp.bfloat16),
                 pltpu.VMEM((model_dim, head_dim), jnp.bfloat16),
                 pltpu.VMEM((model_dim, head_dim), jnp.bfloat16),
@@ -364,14 +380,14 @@
                 pltpu.VMEM((slots, chunk, head_dim), jnp.bfloat16),
                 pltpu.VMEM((slots, head_dim, chunk), jnp.bfloat16),
                 pltpu.SemaphoreType.DMA((rows // RB,)),
-                pltpu.SemaphoreType.DMA((3,)),
+                pltpu.SemaphoreType.DMA((4,)),
                 pltpu.SemaphoreType.DMA((2, rounds, 2)),
                 pltpu.SemaphoreType.DMA((2, rounds, 2)),
                 pltpu.SemaphoreType.DMA((2, rounds + 1, 2)),
                 pltpu.SemaphoreType.DMA((2, rounds + 1, 2)),
             ] + [pltpu.VMEM((2 * chunk, RB), jnp.float32)] * (2 * heads * chunk // RB) + [pltpu.VMEM((SUB, RB), jnp.float32)] * (2 * heads * chunk // RB),
-            compiler_params=pltpu.CompilerParams(collective_id=0, has_side_effects=True, vmem_limit_bytes=47 << 20),
-        )(cos_part, sin_part, *(pltpu.with_memory_space_constraint(a, pltpu.HBM) for a in (hidden, w_k.reshape(model_dim, head_dim), w_v.reshape(model_dim, head_dim), w_q.reshape(model_dim * heads, head_dim))))
+            compiler_params=pltpu.CompilerParams(collective_id=0, has_side_effects=True, vmem_limit_bytes=48 << 20),
+        )(rope_freqs(head_dim), *(pltpu.with_memory_space_constraint(a, pltpu.HBM) for a in (hidden, w_k.reshape(model_dim, head_dim), w_v.reshape(model_dim, head_dim), w_q.reshape(model_dim * heads, head_dim), w_o.reshape(heads * head_dim, model_dim))))
         band = 256
         return pl.pallas_call(
             functools.partial(out_kernel, band),
@@ -380,6 +396,6 @@
             in_specs=[vmem, vmem],
             out_specs=pl.BlockSpec((band, model_dim), lambda j: (j, 0)),
             compiler_params=pltpu.CompilerParams(vmem_limit_bytes=24 << 20),
-        )(attended, w_o.reshape(heads * head_dim, model_dim))
+        )(attended, w_out)
 
     return jax.shard_map(device_step, mesh=mesh, in_specs=(P(('dp', 'cp'), None), P(), P(), P(), P()), out_specs=P(('dp', 'cp'), None), check_vma=False)

time: 48.9 us -> 47.7 us (0.975)
  other arithmetic: 1.14 us -> 0.01 us
    sin x1 -> x0, other arithmetic: 0.98 us -> none  [rope_tables(): return (jnp.cos(angles), jnp.sin(angles))]
where the time goes in v4:
time: 47.7 us
  Pallas kernels  47.6 us (100%)
    pallas_call x1, Pallas kernels, device_step(): pl.pallas_call(functools.partial(fused_kernel, cp_size, rounds, heads), o...  41.1 us
    pallas_call x1, Pallas kernels, device_step(): pl.pallas_call(functools.partial(out_kernel, band), out_shape=jax.ShapeDt...  6.45 us

profile of v4, /device:TPU:55, one launch (start us, length us, event | category | flops | bytes accessed | tf_op | source)
XLA Modules:
  0.0 47.7 jit_solution(14496159780604468210)
XLA Ops:
  0.0 0.1 broadcast_in_dim.2.freq_ref
  0.1 41.1 %shard_map.55 = (bf16[1024,512]{1,0:T(8,128)(2,1)S(1)}, bf16[512,4096]{1,0:T(8,128)(2,1)S(1)}) custom-call(f32[64,128]{1,0:T(8,128)S(1)} %broadcast_in_dim.2.freq_ref, bf16[1024,4096]{1,0:T(8,128)(2,1)} %x_hbm.1, bf16[4096,128]{1,0:T(8,128)(2,1)} %bitcast.6, bf16[4096,128]{1,0:T(8,128)(2,1)} %bitcast.7, bf16[16384,128]{1,0:T(8,128)(2,1)} %bitcast.4, ...), custom_call_target="tpu_custom_call" | custom-call | tf_op jit(solution)/shard_map/pallas_call | solution.py:362
  41.2 6.5 %shard_map.56 = bf16[1024,4096]{1,0:T(8,128)(2,1)} custom-call(bf16[1024,512]{1,0:T(8,128)(2,1)S(1)} %get-tuple-element.7.o_ref, bf16[512,4096]{1,0:T(8,128)(2,1)S(1)} %get-tuple-element.8.w_ref), custom_call_target="tpu_custom_call" | custom-call | tf_op jit(solution)/shard_map/pallas_call | solution.py:392
  (1 shorter events, 0.0 us)

commit v5 on v4

--- a/solution.py
+++ b/solution.py
@@ -343,9 +343,17 @@
             pl.when(own_push[n])(sib(n, 0, kv).wait_send)
 
 
-def out_kernel(band, o_ref, w_ref, y_ref):
-    rows = pl.ds(pl.multiple_of(pl.program_id(0) * band, band), band)
-    y_ref[...] = jnp.dot(o_ref[rows, :], w_ref[...], preferred_element_type=jnp.float32).astype(jnp.bfloat16)
+def out_kernel(bands, halves, o_ref, w_ref, y_hbm, y_buf, y_sem):
+    rows, cols = y_buf.shape[0] // bands, y_buf.shape[1] // halves
+    copies = []
+    for i in range(bands):
+        for j in range(halves):
+            at = (slice(i * rows, (i + 1) * rows), slice(j * cols, (j + 1) * cols))
+            y_buf[at] = jnp.dot(o_ref[at[0], :], w_ref[:, at[1]], preferred_element_type=jnp.float32).astype(jnp.bfloat16)
+            copies.append(pltpu.make_async_copy(y_buf.at[at], y_hbm.at[at], y_sem.at[i, j]))
+            copies[-1].start()
+    for copy in copies:
+        copy.wait()
 
 
 def solution(mesh):
@@ -388,13 +396,13 @@
             ] + [pltpu.VMEM((2 * chunk, RB), jnp.float32)] * (2 * heads * chunk // RB) + [pltpu.VMEM((SUB, RB), jnp.float32)] * (2 * heads * chunk // RB),
             compiler_params=pltpu.CompilerParams(collective_id=0, has_side_effects=True, vmem_limit_bytes=48 << 20),
         )(rope_freqs(head_dim), *(pltpu.with_memory_space_constraint(a, pltpu.HBM) for a in (hidden, w_k.reshape(model_dim, head_dim), w_v.reshape(model_dim, head_dim), w_q.reshape(model_dim * heads, head_dim), w_o.reshape(heads * head_dim, model_dim))))
-        band = 256
+        bands, halves = 4, 2
         return pl.pallas_call(
-            functools.partial(out_kernel, band),
+            functools.partial(out_kernel, bands, halves),
             out_shape=jax.ShapeDtypeStruct((rows, model_dim), jnp.bfloat16),
-            grid=(rows // band,),
             in_specs=[vmem, vmem],
-            out_specs=pl.BlockSpec((band, model_dim), lambda j: (j, 0)),
+            out_specs=hbm,
+            scratch_shapes=[pltpu.VMEM((rows, model_dim), jnp.bfloat16), pltpu.SemaphoreType.DMA((bands, halves))],
             compiler_params=pltpu.CompilerParams(vmem_limit_bytes=24 << 20),
         )(attended, w_out)
 

time: 47.7 us -> 47 us (0.985)
  Pallas kernels: 47.6 us -> 46.7 us
    pallas_call x1, Pallas kernels: 6.45 us -> 5.59 us  [device_step(): pl.pallas_call(functools.partial(out_kernel, bands, halves), out_shape=ja...]
where the time goes in v5:
time: 47 us
  Pallas kernels  46.7 us (99%)
    pallas_call x1, Pallas kernels, device_step(): pl.pallas_call(functools.partial(fused_kernel, cp_size, rounds, heads), o...  41.1 us
    pallas_call x1, Pallas kernels, device_step(): pl.pallas_call(functools.partial(out_kernel, bands, halves), out_shape=ja...  5.59 us

profile of v5, /device:TPU:55, one launch (start us, length us, event | category | flops | bytes accessed | tf_op | source)
XLA Modules:
  0.0 47.0 jit_solution(6471088768816101027)
XLA Ops:
  0.0 0.1 broadcast_in_dim.2.freq_ref
  0.1 41.1 %shard_map.55 = (bf16[1024,512]{1,0:T(8,128)(2,1)S(1)}, bf16[512,4096]{1,0:T(8,128)(2,1)S(1)}) custom-call(f32[64,128]{1,0:T(8,128)S(1)} %broadcast_in_dim.2.freq_ref, bf16[1024,4096]{1,0:T(8,128)(2,1)} %x_hbm.1, bf16[4096,128]{1,0:T(8,128)(2,1)} %bitcast.6, bf16[4096,128]{1,0:T(8,128)(2,1)} %bitcast.7, bf16[16384,128]{1,0:T(8,128)(2,1)} %bitcast.4, ...), custom_call_target="tpu_custom_call" | custom-call | tf_op jit(solution)/shard_map/pallas_call | solution.py:370
  41.2 5.6 %shard_map.56 = bf16[1024,4096]{1,0:T(8,128)(2,1)} custom-call(bf16[1024,512]{1,0:T(8,128)(2,1)S(1)} %get-tuple-element.7.o_ref, bf16[512,4096]{1,0:T(8,128)(2,1)S(1)} %get-tuple-element.8.w_ref), custom_call_target="tpu_custom_call" | custom-call | tf_op jit(solution)/shard_map/pallas_call | solution.py:400
  (1 shorter events, 0.0 us)
